TPU v7x, 128 devices: a whole 4x4x4 slice. The times are simulated.
128 devices in a mesh: ep: 32 (over x, z, core), etp: 4 (over y).
Axes of the slice: x: 4, y: 4, z: 4, core: 2. Of those that a mesh axis runs over, the one named last changes fastest.
Arguments:
- tokens: bfloat16 [4096, 4096], P('ep', 'etp'), may hold values from -6 to 6
- expert_ids: int32 [4096, 8], P('ep'), may hold values from 0 to 63, all different within a row; in each aligned block of 128 rows (0 to 127, 128 to 255, ...) at most 24 rows name the same one
- gate_prob: float32 [4096, 8], P('ep'), may hold values from 0.05 to 1
- gate_weight: bfloat16 [64, 4096, 1536], P('ep', None, 'etp'), may hold values from -0.09375 to 0.09375
- up_weight: bfloat16 [64, 4096, 1536], P('ep', None, 'etp'), may hold values from -0.09375 to 0.09375
- down_weight: bfloat16 [64, 1536, 4096], P('ep', 'etp'), may hold values from -0.15625 to 0.15625
Outputs:
- mixed: bfloat16 [4096, 4096], P('ep', 'etp')
Inputs may be any that keep to these rules, and one draw needn't show every extreme that they name: `expert_ids`: each row names 8 different experts. Within each aligned block of 128 rows (one token group) no expert is named more than 24 times, and in every draw some expert is named exactly 24 times in some block.
All inputs are finite; a program needn't handle non-finite values.
Results may differ from a plain program's by a relative error of at most 0.012.
Values may be sent and summed in bfloat16 or wider, within the bound.
A program may use at most 128 MiB of HBM per device.

v0:
```python
import jax
import jax.numpy as jnp
from jax import lax
from jax.sharding import PartitionSpec as P


def body(tokens, expert_ids, gate_prob, gate_weight, up_weight, down_weight):
    groups = lax.axis_size("ep")
    local_experts = gate_weight.shape[0]
    experts = local_experts * groups
    tok_rows = expert_ids.shape[0]
    fanout = expert_ids.shape[1]
    capacity = max(2, 3 * tok_rows * fanout // (2 * experts))
    flat_ids = expert_ids.reshape(-1)
    onehot = (flat_ids[:, None] == jnp.arange(experts, dtype=jnp.int32)[None, :]).astype(jnp.int32)
    position = jnp.sum((jnp.cumsum(onehot, axis=0) - onehot) * onehot, axis=1)
    slot_index = flat_ids * capacity + position
    owners = jnp.arange(tok_rows * fanout, dtype=jnp.int32) // fanout
    source = jnp.full((experts * capacity,), tok_rows, jnp.int32).at[slot_index].set(owners)
    features = lax.all_gather(tokens, "etp", axis=1, tiled=True)
    padded = jnp.concatenate([features, jnp.zeros((1, features.shape[1]), features.dtype)], axis=0)
    outgoing = padded[source].reshape(groups, local_experts, capacity, features.shape[1])
    arrived = lax.all_to_all(outgoing, "ep", split_axis=0, concat_axis=2, tiled=True)
    partials = []
    for member in range(local_experts):
        expert_rows = arrived[0, member]
        gate_sum = jnp.dot(expert_rows, gate_weight[member], preferred_element_type=jnp.float32)
        up_sum = jnp.dot(expert_rows, up_weight[member], preferred_element_type=jnp.float32)
        hidden = (jax.nn.silu(gate_sum) * up_sum).astype(jnp.bfloat16)
        partials.append(jnp.dot(hidden, down_weight[member], preferred_element_type=jnp.float32))
    partial_all = jnp.stack(partials).reshape(local_experts, groups, capacity, down_weight.shape[2])
    combine_scale = gate_prob.reshape(tok_rows, fanout, 1)
    summed = lax.psum_scatter(
        partial_all.astype(jnp.bfloat16), "etp", scatter_dimension=3, tiled=True
    ).astype(jnp.float32)
    returned = lax.all_to_all(
        summed.astype(jnp.bfloat16), "ep", split_axis=1, concat_axis=0, tiled=True
    ).astype(summed.dtype)
    picked = returned.reshape(experts * capacity, -1)[slot_index].reshape(tok_rows, fanout, -1)
    mixed = jnp.sum(picked * combine_scale, axis=1).astype(jnp.bfloat16)
    return mixed


def solution(mesh):
    in_specs = (
        P("ep", "etp"),
        P("ep", None),
        P("ep", None),
        P("ep", None, "etp"),
        P("ep", None, "etp"),
        P("ep", "etp", None),
    )
    out_specs = P("ep", "etp")
    return jax.shard_map(body, mesh=mesh, in_specs=in_specs, out_specs=out_specs, check_vma=False)
```

profile of v0, /device:TPU:0, one launch (start us, length us, event | category | flops | bytes accessed | tf_op | source)
XLA Modules:
  0.0 410.2 jit_solution(12955724353546983970)
XLA Ops:
  6.5 0.7 all-gather.2.cloned.1.call-update
  7.3 0.8 copy.17
  8.3 18.0 %reduce-window.6 = s32[64,8,128]{2,1,0:T(8,128)S(1)} reduce-window(s32[64,8,128]{2,1,0:T(8,128)S(1)} %fusion.34, s32[]{:T(128)} %constant.32.clone.1), window={size=1x1x128 pad=0_0x0_0x127_0}, to_apply=%region_0.0 | reduce-window | flops 8323072 | bytes 524292 | tf_op jit(solution)/shard_map/reduce-window
  26.7 0.7 broadcast_multiply_fusion
  27.9 4.3 %scatter_custom_fusion = s32[1536]{0:T(1024)S(1)} fusion(s32[1024]{0:T(1024)S(1)} %bitcast.97, s32[1024]{0:T(1024)S(1)} %add_select_fusion, s32[]{:T(128)} %constant.30.clone.1), kind=kCustom, calls=%fused_computation.50 | custom fusion | bytes 6148 | tf_op jit(solution)/shard_map/scatter | solution.py:19
  32.2 3.5 all-gather.2.cloned.1.call-done
  35.7 1.3 concatenate.5
  37.0 9.5 %gather_fusion = bf16[1536,4096]{1,0:T(8,128)(2,1)} fusion(bf16[129,4096]{1,0:T(8,128)(2,1)S(1)} %concatenate.5, s32[2048]{0:T(1024)S(1)} %pad_clamp_fusion), kind=kCustom, calls=%fused_computation | custom fusion | bytes 25171968 | tf_op jit(solution)/shard_map/gather | solution.py:22
  46.6 147.8 %all_to_all.27 = bf16[32,2,24,4096]{3,2,1,0:T(8,128)(2,1)S(1)} all-to-all(bf16[32,2,24,4096]{3,2,1,0:T(8,128)(2,1)} %bitcast.89), channel_id=1, replica_groups=mesh['ep'=32,'etp'=4] {'ep'}, dimensions={0} | all-to-all | bytes 25165824 | tf_op jit(solution)/shard_map/all_to_all | solution.py:23
  194.4 1.9 copy.21
  196.3 3.4 fusion.3
  199.8 3.4 fusion.5
  203.2 3.5 fusion.25
  206.7 3.5 fusion.28
  210.2 3.7 fusion
  213.9 3.9 fusion.1
  217.7 5.5 %pad_maximum_fusion = bf16[2,32,24,4096]{3,2,1,0:T(8,128)(2,1)} fusion(bf16[1,32,24,4096]{3,2,1,0:T(8,128)(2,1)S(1)} %fusion.1, bf16[1,32,24,4096]{3,2,1,0:T(8,128)(2,1)S(1)} %fusion), kind=kLoop, calls=%fused_computation.3 | loop fusion | flops 6291456 | bytes 25165824 | tf_op jit(solution)/shard_map/stack | solution.py:31
  223.3 111.9 %reduce-scatter.2.cloned.1.call-done = bf16[2,32,24,1024]{3,2,1,0:T(8,128)(2,1)} async-done(((bf16[2,32,24,4096]{3,2,1,0:T(8,128)(2,1)}), bf16[2,32,24,1024]{3,2,1,0:T(8,128)(2,1)}) %reduce-scatter.2.cloned.1.call-update) | async-done | bytes 3145744 | tf_op jit(solution)/shard_map/reduce_scatter | solution.py:33
  335.1 4.0 copy.22
  339.1 7.2 %all-to-all-start.1 = ((bf16[2,32,24,1024]{3,2,0,1:T(8,128)(2,1)}), bf16[2,32,24,1024]{3,2,0,1:T(8,128)(2,1)S(1)}, u32[]{:S(2)}, u32[]{:S(2)}) async-start(bf16[2,32,24,1024]{3,2,0,1:T(8,128)(2,1)} %copy.22), calls=%async_computation.2 | async-start | bytes 6291456 | tf_op jit(solution)/shard_map/all_to_all | solution.py:36
  346.5 40.0 %all-to-all-done.1 = bf16[2,32,24,1024]{3,2,0,1:T(8,128)(2,1)S(1)} async-done(((bf16[2,32,24,1024]{3,2,0,1:T(8,128)(2,1)}), bf16[2,32,24,1024]{3,2,0,1:T(8,128)(2,1)S(1)}, u32[]{:S(2)}, u32[]{:S(2)}) %all-to-all-start.1) | async-done | bytes 3145760 | tf_op jit(solution)/shard_map/all_to_all | solution.py:36
  386.5 3.4 bitcast_convert_fusion
  390.0 9.2 %gather_fusion.1 = f32[1024,1024]{1,0:T(8,128)} fusion(f32[1536,1024]{1,0:T(8,128)} %bitcast.88, s32[1024]{0:T(1024)S(1)} %broadcast_clamp_fusion), kind=kCustom, calls=%fused_computation.1 | custom fusion | bytes 8392704 | tf_op jit(solution)/shard_map/gather | solution.py:39
  399.2 4.2 %fusion.6 = bf16[128,1024]{1,0:T(8,128)(2,1)} fusion(f32[1024,1024]{1,0:T(8,128)} %gather_fusion.1, f32[128,8]{1,0:T(8,128)S(1)} %copy.23), kind=kLoop, calls=%fused_computation.15 | loop fusion | flops 1966080 | bytes 4460544 | tf_op jit(solution)/shard_map/reduce_sum | solution.py:40
  (38 shorter events, 1.2 us)
Async XLA Ops:
  6.5 29.2 %all-gather.2.cloned.1.call-start = ((), (), s32[]{:S(2)}) async-start(), calls=%async_computation.3 | async-start | bytes 1310720 | tf_op jit(solution)/shard_map/all_gather | solution.py:20
  7.3 327.9 %reduce-scatter.2.cloned.1.call-start = ((), (), s32[]{:S(2)}) async-start(), calls=%async_computation.4 | async-start | bytes 15728640 | tf_op jit(solution)/shard_map/reduce_scatter | solution.py:33
  46.6 149.7 %slice-start = ((s8[6291456]{0:T(1024)(128)(4,1)}), s8[4194304]{0:T(1024)(128)(4,1)S(1)}, s32[]{:S(2)}) async-start(s8[6291456]{0:T(1024)(128)(4,1)} %bitcast.99), calls=%async_computation.5 | async-start | bytes 8388608
  194.4 1.9 slice-start.1
  196.3 6.8 %slice-start.2 = ((s8[6291456]{0:T(1024)(128)(4,1)}), s8[4194304]{0:T(1024)(128)(4,1)S(1)}, s32[]{:S(2)}) async-start(s8[6291456]{0:T(1024)(128)(4,1)} %bitcast.101), calls=%async_computation.7 | async-start | bytes 8388608
  199.7 3.4 slice-start.3
  203.2 7.0 %slice-start.4 = ((s8[6291456]{0:T(1024)(128)(4,1)}), s8[4194304]{0:T(1024)(128)(4,1)S(1)}, s32[]{:S(2)}) async-start(s8[6291456]{0:T(1024)(128)(4,1)} %bitcast.103), calls=%async_computation.9 | async-start | bytes 8388608
  206.7 3.5 slice-start.5
  223.3 123.1 %copy-start = (f32[128,8]{0,1:T(8,128)S(1)}, f32[128,8]{0,1:T(8,128)}, u32[]{:S(2)}) copy-start(f32[128,8]{0,1:T(8,128)} %param.8) | copy-start | bytes 12292
  339.1 47.4 %all-to-all-start.1 = ((bf16[2,32,24,1024]{3,2,0,1:T(8,128)(2,1)}), bf16[2,32,24,1024]{3,2,0,1:T(8,128)(2,1)S(1)}, u32[]{:S(2)}, u32[]{:S(2)}) async-start(bf16[2,32,24,1024]{3,2,0,1:T(8,128)(2,1)} %copy.22), calls=%async_computation.2 | async-start | bytes 6291456 | tf_op jit(solution)/shard_map/all_to_all | solution.py:36
Sparse Core Ops, SparseCore 0:
  9.0 26.6 all-gather.1
  223.4 111.7 reduce-scatter.1
where the time goes:
time: 411 us; the launch traced here: 410 us
  waiting for transfers between devices  156 us (38%)
  blocking collectives  148 us (36%)
  other arithmetic  32.1 us (8%)
  local copies, waits for them, and re-layouts  31.9 us (8%)
  matrix products  21.3 us (5%)
  between operations  13.7 us (3%)
  starting transfers between devices  7.29 us (2%)
    all_to_all x1, blocking collectives, body(): lax.all_to_all(outgoing, 'ep', split_axis=0, concat_axis=2, tiled=True)  148 us
    reduce_scatter x1, waiting for transfers between devices, body(): lax.psum_scatter(partial_all.astype(jnp.bfloat16), 'etp', scatter_dimensi...  112 us
    all_to_all x1, waiting for transfers between devices, body(): lax.all_to_all(summed.astype(jnp.bfloat16), 'ep', split_axis=1, concat_ax...  40 us
    another operation x3, other arithmetic  18.2 us
    gather x1, local copies, waits for them, and re-layouts, body(): padded[source].reshape(groups, local_experts, capacity, features.shape[1])  9.53 us
    gather x1, local copies, waits for them, and re-layouts, body(): returned.reshape(experts * capacity, -1)[slot_index]  9.2 us
  transfers between devices with their start and end apart: 3, of which 3 were waited for; matrix products, arithmetic and copies ran while one was open for 6% of the time, Pallas kernels for 0%

commit v1 on v0

v1 whole, which is shorter than its diff:
```python
import heapq

import jax
import jax.numpy as jnp
from jax import lax
from jax.experimental import pallas as pl
from jax.experimental.pallas import tpu as pltpu
from jax.sharding import PartitionSpec as P

MESH = pl.DeviceIdType.MESH
F32 = jnp.float32
BF16 = jnp.bfloat16
X, Y, Z = 0, 1, 2
ORDERS = (
    (Y, Z, X), (X, Z, Y), (X, Y, Z),
    (Y, Z, X), (X, Z, Y), (Y, X, Z),
    (Y, Z, X), (X, Z, Y),
)
NP = len(ORDERS)
CAP = 24
PAIR = 2 * CAP


def plan():
    rate, lat = 46.6e3, 2.2
    free = {}
    arrive = {}
    done = {}
    tasks = {}

    def size(ph):
        return 16384 * 4 ** ph

    def add(name, prio, cost, after=(), needs=(), sends=()):
        tasks[name] = (prio, cost, after, needs, sends)

    for j, order in enumerate(ORDERS):
        for ph in range(3):
            a, k = order[ph], (j, ph)
            before = [("AD", j, ph - 1)] if ph else []
            s = size(ph)
            add(("AS", j, ph), (0, j, ph, 0), 0.05, before, (),
                [(a, 1, s, ("ga+",) + k), (a, -1, s, ("ga-",) + k), (a, 1, s, ("gc1",) + k), (a, -1, s, ("gc2",) + k)])
            add(("AF+", j, ph), (0, j, ph, 1), 0.05, [("AS", j, ph)], [("ga+",) + k], [(a, 1, s, ("gc3",) + k)])
            add(("AF-", j, ph), (0, j, ph, 2), 0.05, [("AS", j, ph)], [("ga-",) + k], [(a, -1, s, ("gc4",) + k)])
            add(("AD", j, ph), (0, j, ph, 3), 0.05, [("AF+", j, ph), ("AF-", j, ph)], [(f"gc{i}",) + k for i in (1, 2, 3, 4)])
        add(("LW", j), (1, j), 0.1, [("GU", j - 2)] if j >= 2 else [], [("pw", j)])
        add(("SEL", j), (3, j, 0), 0.9, [("AD", j, 2), ("ST",)] + ([("GU", j - 1)] if j else []))
        add(("GU", j), (3, j, 1), 2.2, [("SEL", j), ("LW", j)])
        add(("DW", j), (1, j), 0.1, [("CB", j - 2)] if j >= 2 else [("LW", NP - 1)], [("pd",)])
        add(("DN", j), (3, 10 + j, 1), 1.2, [("HID",), ("DW", j)] + ([("CB", j - 1)] if j else []))
        add(("CB", j), (3, 10 + j, 2), 1.0, [("DN", j)])
        for r in range(3):
            ph = 2 - r
            a, k = order[ph], (j, ph)
            s = size(ph)
            v = 0.02 + 0.15 * s / 262144
            add(("RS", j, ph), (0, 10 + j, r, 0), 0.05, [("RD", j, ph + 1)] if r else [("CB", j)], (),
                [(a, 1, s, ("ra+",) + k), (a, -1, s, ("ra-",) + k), (a, 1, s, ("rc1",) + k), (a, -1, s, ("rc2",) + k)])
            add(("RF+", j, ph), (0, 10 + j, r, 1), v, [("RS", j, ph)], [("ra+",) + k], [(a, 1, s, ("rc3",) + k)])
            add(("RF-", j, ph), (0, 10 + j, r, 2), v, [("RS", j, ph)], [("ra-",) + k], [(a, -1, s, ("rc4",) + k)])
            add(("RD", j, ph), (0, 10 + j, r, 3), 2 * v, [("RF+", j, ph), ("RF-", j, ph)], [(f"rc{i}",) + k for i in (1, 2, 3, 4)])
    add(("META",), (2, 0), 1.0, (), [("meta",)])
    for q in range(NP):
        add(("SB", q), (2, 1 + q), 0.6, [("META",)])
    add(("ST",), (2, 20), 0.0, [("SB", q) for q in range(NP)])
    add(("HID",), (3, 9), 1.5, [("GU", NP - 1)])
    arrive[("meta",)] = 5.0
    for j in range(NP):
        arrive[("pw", j)] = 4.0 + 4.5 * (j + 1)
    arrive[("pd",)] = 4.0 + 4.5 * NP + 14

    now, out = 0.0, []
    while tasks:
        ready, later = [], []
        for name, (prio, cost, after, needs, sends) in tasks.items():
            if all(d in done for d in after) and all(n in arrive for n in needs):
                t = max([0.0] + [arrive[n] for n in needs])
                if t <= now:
                    ready.append((prio, name))
                else:
                    later.append((t, prio, name))
        if not ready:
            now = min(later)[0]
            continue
        name = min(ready)[1]
        prio, cost, after, needs, sends = tasks.pop(name)
        now += cost
        for a, d, s, tag in sends:
            begin = max(now, free.get((a, d), 0.0))
            free[(a, d)] = begin + s / rate
            arrive[tag] = begin + s / rate + lat
        done[name] = now
        out.append(name)
    return out, now


SCHEDULE, PLANNED_US = plan()


def half_shape(order, ph):
    full = order[:ph]
    return (4 if X in full else 1, 4 if Z in full else 1, 64, 512 if Y in full else 128)


def kernel(tok, meta, gw, uw, dw, out, pw, pd, t_ref, w_ref, d_ref, x_ref, acc, hid, y_ref, s_ref, st_ref, ps, rk, pr, mb,
           ga, gc, gs, ra, rc, rs, tok_sem, meta_send, meta_recv, meta_own, pw_send, pw_recv, pd_send, pd_recv,
           w_sem, d_sem, *rb):
    ep = lax.axis_index("ep")
    y = lax.axis_index("etp")
    x, z, core = ep // 8, (ep // 2) % 4, ep % 2
    own = (x, y, z)

    def at(axis, delta):
        c = [x, y, z]
        c[axis] = (c[axis] + delta + 4) % 4
        return {"ep": c[X] * 8 + c[Z] * 2 + core, "etp": c[Y]}

    partner = {"ep": x * 8 + z * 2 + (1 - core), "etp": y}
    plane = [
        {"ep": ((x + dx) % 4) * 8 + ((z + dz) % 4) * 2 + core, "etp": y}
        for dx in range(4) for dz in range(4) if dx or dz
    ]

    own_tok = [
        pltpu.make_async_copy(
            tok.at[:, pl.ds(j * 128, 128)],
            t_ref.at[j, x, z, :, pl.ds(pl.multiple_of(y * 128, 128), 128)], tok_sem.at[j])
        for j in range(NP)
    ]
    for c in own_tok:
        c.start()
    g = x * 4 + z
    own_meta = pltpu.make_async_copy(meta, mb.at[g], meta_own)
    own_meta.start()

    barrier = pltpu.get_barrier_semaphore()
    greet = plane + [at(Y, 1), at(Y, -1), partner]
    for d in greet:
        pl.semaphore_signal(barrier, inc=1, device_id=d, device_id_type=MESH)
    pl.semaphore_wait(barrier, len(greet))

    def remote(src, dst, ssem, rsem, dev):
        pltpu.make_async_remote_copy(src_ref=src, dst_ref=dst, send_sem=ssem, recv_sem=rsem,
                                     device_id=dev, device_id_type=MESH).start()

    def wait(ref, sem):
        pltpu.make_async_copy(ref, ref, sem).wait()

    def slab(j, ph, pos, half=None, many=1):
        order = ORDERS[j]
        a, full = order[ph], order[:ph]

        def pick(axis):
            if axis in full:
                return pl.ds(0, 4)
            if axis == a:
                return pl.ds(pos, many)
            return pl.ds(own[axis], 1)

        cy = pick(Y)
        cols = pl.ds(0, 512) if Y in full else pl.ds(
            pl.multiple_of((pos if Y == a else y) * 128, 128), 128 * (many if Y == a else 1))
        rows = pl.ds(0, 128) if half is None else pl.ds(64 * half, 64)
        return t_ref.at[j, pick(X), pick(Z), rows, cols]

    def place(j, ph, delta):
        return (own[ORDERS[j][ph]] + delta + 4) % 4

    def run_as(j, ph):
        if ph == 0:
            own_tok[j].wait()
        a, p = ORDERS[j][ph], own[ORDERS[j][ph]]
        fwd, bwd = at(a, 1), at(a, -1)
        for half, sem_f in ((0, ga.at[j, ph, 0]), (1, gc.at[j, ph])):
            h = slab(j, ph, p, half)
            remote(h, h, gs.at[j, ph], sem_f, fwd)
            o = slab(j, ph, p, 1 - half)
            remote(o, o, gs.at[j, ph], ga.at[j, ph, 1] if half == 0 else gc.at[j, ph], bwd)

    def run_af(j, ph, sign):
        a = ORDERS[j][ph]
        half = 0 if sign > 0 else 1
        ref = slab(j, ph, place(j, ph, -sign), half)
        wait(ref, ga.at[j, ph, half])
        remote(ref, ref, gs.at[j, ph], gc.at[j, ph], at(a, sign))

    def run_ad(j, ph):
        wait(slab(j, ph, 0, None, 2), gc.at[j, ph])

    def run_lw(j):
        wait(pw.at[j], pw_recv.at[j])
        slot = j % 2
        for e, base in ((0, None), (1, pw)):
            for m, src in ((0, gw), (1, uw)):
                s = src.at[:, :, j] if base is None else pw.at[j, m]
                pltpu.make_async_copy(s, w_ref.at[slot, pl.ds(2 * e, 2), :, :, pl.ds(m * 384, 384)], w_sem.at[slot]).start()

    def run_dw(j):
        if j == 0:
            wait(pd, pd_recv)
        slot = j % 2
        for e, src in ((0, dw), (1, pd)):
            for k in range(4):
                pltpu.make_async_copy(
                    src.at[:, :, pl.ds(k * 1024 + j * 128, 128)],
                    d_ref.at[slot, pl.ds(2 * e, 2), :, pl.ds(k * 128, 128)], d_sem.at[slot]).start()

    def run_meta():
        own_meta.wait()
        wait(mb.at[pl.ds(0, 15)], meta_recv)
        ids = mb[:, 0:8, :]
        probs = mb[:, 8:16, :]
        chip = (x * 4 + z) * 4
        first = [chip + 2 * core, chip + 2 * core + 1, chip + 2 * (1 - core), chip + 2 * (1 - core) + 1]
        rows, prows = [], []
        for e in first:
            hit = ids == e.astype(F32)
            rows.append(jnp.sum(jnp.where(hit, 1.0, 0.0), axis=1))
            prows.append(jnp.sum(jnp.where(hit, probs, 0.0), axis=1))
        ind = jnp.concatenate(rows, axis=0)
        pr[...] = jnp.concatenate(prows, axis=0)
        upper = (lax.broadcasted_iota(jnp.int32, (128, 128), 0) < lax.broadcasted_iota(jnp.int32, (128, 128), 1))
        rank = jnp.dot(ind.astype(BF16), jnp.where(upper, 1.0, 0.0).astype(BF16), preferred_element_type=F32)
        odd = (lax.broadcasted_iota(jnp.int32, (64, 128), 0) % 2).astype(F32) * float(CAP)
        rk[...] = jnp.where(ind > 0.5, rank + odd, -1.0)

    def run_sb(q):
        row = lax.broadcasted_iota(jnp.int32, (PAIR, 128), 0).astype(F32)
        blocks = []
        for e in range(4):
            i = e * 16 + 2 * q
            left = jnp.where(row == rk[i:i + 1, :], 1.0, 0.0)
            right = jnp.where(row == rk[i + 1:i + 2, :], 1.0, 0.0)
            ps[e, q * PAIR:(q + 1) * PAIR, :] = jnp.sum(
                left * pr[i:i + 1, :] + right * pr[i + 1:i + 2, :], axis=1, keepdims=True)
            blocks.append(jnp.concatenate([left, right], axis=1))
        blocks.append(jnp.zeros((256 - 4 * PAIR, 256), F32))
        full = jnp.concatenate(blocks, axis=0)
        s_ref[q] = full[:4 * PAIR].astype(BF16)
        st_ref[q] = full.T.astype(BF16)
        y_ref[q, 4 * PAIR:, :] = jnp.zeros((256 - 4 * PAIR, 512), BF16)

    def run_sel(j):
        def step(i, carry):
            for k in range(4):
                q = 4 * i + k
                t = t_ref[j, 2 * i + k // 2, (k % 2) * 2:(k % 2) * 2 + 2].reshape(256, 512)
                r = jnp.dot(s_ref[q], t, preferred_element_type=F32).astype(BF16)
                for e in range(4):
                    x_ref[e, pl.ds(pl.multiple_of(q * PAIR, 16), PAIR), :] = r[e * PAIR:(e + 1) * PAIR]
            return carry

        lax.fori_loop(0, 2, step, 0)

    def run_gu(j):
        slot = j % 2
        wait(w_ref.at[slot], w_sem.at[slot])

        def step(e, carry):
            for n in range(3):
                w = w_ref[slot, e, :, :, n * 256:(n + 1) * 256].reshape(512, 256)
                r = jnp.dot(x_ref[e], w, preferred_element_type=F32)
                if j == 0:
                    acc[e, :, n * 256:(n + 1) * 256] = r
                else:
                    acc[e, :, n * 256:(n + 1) * 256] += r
            return carry

        lax.fori_loop(0, 4, step, 0)

    def run_hid():
        def step(i, carry):
            e, k = i // 8, i % 8
            rows = pl.ds(pl.multiple_of(k * 48, 16), 48)
            gate, up = acc[e, rows, 0:384], acc[e, rows, 384:768]
            h = gate / (1.0 + jnp.exp(-gate)) * up * ps[e, rows, :]
            hid[e, rows, :] = h.astype(BF16)
            return carry

        lax.fori_loop(0, 32, step, 0)

    def run_dn(j):
        slot = j % 2
        wait(d_ref.at[slot], d_sem.at[slot])

        def step(e, carry):
            r = jnp.dot(hid[e], d_ref[slot, e], preferred_element_type=F32).astype(BF16)
            for q in range(NP):
                y_ref[q, pl.ds(pl.multiple_of(e * PAIR, 16), PAIR), :] = r[q * PAIR:(q + 1) * PAIR]
            return carry

        lax.fori_loop(0, 4, step, 0)

    def run_cb(j):
        for ph in range(3):
            wait(slab(j, ph, 0, None, 3), gs.at[j, ph])

        def step(i, carry):
            for k in range(4):
                q = 4 * i + k
                r = jnp.dot(st_ref[q], y_ref[q], preferred_element_type=F32).astype(BF16)
                t_ref[j, 2 * i + k // 2, (k % 2) * 2:(k % 2) * 2 + 2] = r.reshape(2, 128, 512)
            return carry

        lax.fori_loop(0, 2, step, 0)

    def buf(j, ph):
        return rb[3 * j + ph]

    def run_rs(j, ph):
        a = ORDERS[j][ph]
        fwd, bwd = at(a, 1), at(a, -1)
        b, s = buf(j, ph), rs.at[j, ph]
        far = place(j, ph, 2)
        remote(slab(j, ph, far, 0), b.at[0], s, ra.at[j, ph, 0], fwd)
        remote(slab(j, ph, far, 1), b.at[1], s, ra.at[j, ph, 1], bwd)
        remote(slab(j, ph, place(j, ph, 1), 1), b.at[2], s, rc.at[j, ph], fwd)
        remote(slab(j, ph, place(j, ph, -1), 0), b.at[3], s, rc.at[j, ph], bwd)

    def add_into(j, ph, pos, half, parts, last=False):
        b = buf(j, ph)
        nx, nz, _, cols = half_shape(ORDERS[j], ph)
        a, full = ORDERS[j][ph], ORDERS[j][:ph]

        def index(axis, i):
            return i if axis in full else (pos if axis == a else own[axis])

        cpos = 0 if Y in full else pl.multiple_of((pos if a == Y else y) * 128, 128)
        rows = pl.ds(64 * half, 64)

        def step(i, carry):
            ix, iz = i // nz, i % nz
            spot = (j, index(X, ix), index(Z, iz), rows, pl.ds(cpos, cols))
            v = t_ref[spot].astype(F32)
            for k in parts:
                v = v + b[k, ix, iz].astype(F32)
            v = v.astype(BF16)
            if last:
                out[rows, j * 128:(j + 1) * 128] = v
            else:
                t_ref[spot] = v
            return carry

        if nx * nz == 1:
            step(0, 0)
        else:
            lax.fori_loop(0, nx * nz, step, 0)

    def run_rf(j, ph, sign):
        a, b = ORDERS[j][ph], buf(j, ph)
        half = 0 if sign > 0 else 1
        wait(b.at[half], ra.at[j, ph, half])
        pos = place(j, ph, sign)
        add_into(j, ph, pos, half, (half,))
        remote(slab(j, ph, pos, half), b.at[4 + half], rs.at[j, ph], rc.at[j, ph], at(a, sign))

    def run_rd(j, ph):
        b = buf(j, ph)
        wait(b.at[pl.ds(2, 4)], rc.at[j, ph])
        p = own[ORDERS[j][ph]]
        add_into(j, ph, p, 0, (3, 4), ph == 0)
        add_into(j, ph, p, 1, (2, 5), ph == 0)

    started = 0
    while SCHEDULE[started][0] == "AS":
        run_as(*SCHEDULE[started][1:])
        started += 1
    for d in plane:
        remote(meta, mb.at[g], meta_send, meta_recv, d)
    for j in range(NP):
        remote(gw.at[:, :, j], pw.at[j, 0], pw_send, pw_recv.at[j], partner)
        remote(uw.at[:, :, j], pw.at[j, 1], pw_send, pw_recv.at[j], partner)
    remote(dw, pd, pd_send, pd_recv, partner)

    runs = {
        "AS": run_as, "AF+": lambda j, ph: run_af(j, ph, 1), "AF-": lambda j, ph: run_af(j, ph, -1), "AD": run_ad,
        "LW": run_lw, "DW": run_dw, "SEL": run_sel, "GU": run_gu, "DN": run_dn, "CB": run_cb,
        "RS": run_rs, "RF+": lambda j, ph: run_rf(j, ph, 1), "RF-": lambda j, ph: run_rf(j, ph, -1), "RD": run_rd,
        "META": run_meta, "SB": run_sb, "ST": lambda: None, "HID": run_hid,
    }
    for task in SCHEDULE[started:]:
        runs[task[0]](*task[1:])

    for j in range(NP):
        for ph in range(3):
            wait(slab(j, ph, 0, None, 3), rs.at[j, ph])
    wait(mb.at[pl.ds(0, 15)], meta_send)
    wait(pw, pw_send)
    wait(pd, pd_send)


def body(tokens, expert_ids, gate_prob, gate_weight, up_weight, down_weight):
    meta = jnp.concatenate([expert_ids.T.astype(F32), gate_prob.T], axis=0)
    gw = gate_weight.reshape(2, 4, NP, 128, 384)
    uw = up_weight.reshape(2, 4, NP, 128, 384)
    hbm = pl.BlockSpec(memory_space=pl.ANY)
    dma = pltpu.SemaphoreType.DMA
    scratch = [
        pltpu.VMEM((NP, 4, 4, 128, 512), BF16),
        pltpu.VMEM((2, 4, 4, 128, 768), BF16),
        pltpu.VMEM((2, 4, 384, 512), BF16),
        pltpu.VMEM((4, 384, 512), BF16),
        pltpu.VMEM((4, 384, 768), F32),
        pltpu.VMEM((4, 384, 384), BF16),
        pltpu.VMEM((8, 256, 512), BF16),
        pltpu.VMEM((8, 4 * PAIR, 256), BF16),
        pltpu.VMEM((8, 256, 256), BF16),
        pltpu.VMEM((4, 384, 1), F32),
        pltpu.VMEM((64, 128), F32),
        pltpu.VMEM((64, 128), F32),
        pltpu.VMEM((16, 16, 128), F32),
        dma((NP, 3, 2)), dma((NP, 3)), dma((NP, 3)),
        dma((NP, 3, 2)), dma((NP, 3)), dma((NP, 3)),
        dma((NP,)), dma, dma, dma, dma, dma((NP,)), dma, dma, dma((2,)), dma((2,)),
    ] + [pltpu.VMEM((6,) + half_shape(order, ph), BF16) for order in ORDERS for ph in range(3)]
    return pl.pallas_call(
        kernel,
        name="moe",
        out_shape=(
            jax.ShapeDtypeStruct((128, 1024), BF16),
            jax.ShapeDtypeStruct((NP, 2, 2, 4, 128, 384), BF16),
            jax.ShapeDtypeStruct((2, 384, 4096), BF16),
        ),
        in_specs=[hbm] * 5,
        out_specs=(pl.BlockSpec(memory_space=pltpu.VMEM), hbm, hbm),
        scratch_shapes=scratch,
        compiler_params=pltpu.CompilerParams(collective_id=0, has_side_effects=True, vmem_limit_bytes=67043328),
    )(tokens, meta, gw, uw, down_weight)[0]


def solution(mesh):
    in_specs = (
        P("ep", "etp"),
        P("ep", None),
        P("ep", None),
        P("ep", None, "etp"),
        P("ep", None, "etp"),
        P("ep", "etp", None),
    )
    return jax.shard_map(body, mesh=mesh, in_specs=in_specs, out_specs=P("ep", "etp"), check_vma=False)
```

time: 411 us -> 188 us (0.46)
  Pallas kernels: 0 us -> 184 us
  waiting for transfers between devices: 156 us -> 0 us
  blocking collectives: 148 us -> 0 us
  local copies, waits for them, and re-layouts: 31.9 us -> 1.67 us
  other arithmetic: 32.1 us -> 1.97 us
  matrix products: 21.3 us -> 0 us
  between operations: 13.7 us -> 0.01 us
  starting transfers between devices: 7.29 us -> 0 us
    pallas_call x0 -> x1, Pallas kernels: none -> 184 us  [body(): pl.pallas_call(kernel, name='moe', out_shape=(jax.ShapeDtypeStruct((128,...]
    all_to_all x1 -> x0, blocking collectives: 148 us -> none  [body(): lax.all_to_all(outgoing, 'ep', split_axis=0, concat_axis=2, tiled=True)]
    reduce_scatter x1 -> x0, waiting for transfers between devices: 112 us -> none  [body(): lax.psum_scatter(partial_all.astype(jnp.bfloat16), 'etp', scatter_dimensi...]
    all_to_all x1 -> x0, waiting for transfers between devices: 40 us -> none  [body(): lax.all_to_all(summed.astype(jnp.bfloat16), 'ep', split_axis=1, concat_ax...]
    another operation x4 -> x0, other arithmetic: 23.7 us -> none
    dot_general x6 -> x0, matrix products: 21.3 us -> none  [the longest x2 7.54 us: body(): jnp.dot(hidden, down_weight[member], preferred_element_type=jnp.float32)]
    gather x2 -> x0, local copies, waits for them, and re-layouts: 18.7 us -> none  [the longest x1 9.53 us: body(): padded[source].reshape(groups, local_experts, capacity, features.shape[1])]
    all_to_all x1 -> x0, starting transfers between devices: 7.24 us -> none  [body(): lax.all_to_all(summed.astype(jnp.bfloat16), 'ep', split_axis=1, concat_ax...]
  transfers between devices with their start and end apart: 3 -> 0, of which waited for: 3 -> 0; matrix products, arithmetic and copies ran while one was open for 6% -> 0% of each run, Pallas kernels for 0% -> 0%
where the time goes in v1:
time: 188 us
  Pallas kernels  184 us (98%)
  other arithmetic  1.97 us (1%)
    pallas_call x1, Pallas kernels, body(): pl.pallas_call(kernel, name='moe', out_shape=(jax.ShapeDtypeStruct((128,...  184 us

profile of v1, /device:TPU:0, one launch (start us, length us, event | category | flops | bytes accessed | tf_op | source)
XLA Modules:
  0.0 188.0 jit_solution(7280883910696502697)
XLA Ops:
  0.0 0.7 convert_bitcast_fusion
  0.7 1.3 pad_maximum_fusion.meta
  2.0 184.4 %moe.1 = (bf16[128,1024]{1,0:T(8,128)(2,1)}, bf16[8,2,2,4,128,384]{5,4,3,2,1,0:T(8,128)(2,1)}, bf16[2,384,4096]{2,1,0:T(8,128)(2,1)}) custom-call(bf16[128,1024]{1,0:T(8,128)(2,1)} %tok.1, f32[16,128]{1,0:T(8,128)} %pad_maximum_fusion.meta, bf16[2,4,8,128,384]{4,3,2,1,0:T(8,128)(2,1)} %bitcast.5, bf16[2,4,8,128,384]{4,3,2,1,0:T(8,128)(2,1)} %bitcast.6, ...), custom_call_target="tpu_custom_call" | custom-call | tf_op jit(solution)/shard_map/moe/pallas_call | solution.py:417
  186.3 1.7 copy.8

commit v2 on v1

v2 whole, which is shorter than its diff:
```python
import jax
import jax.numpy as jnp
from jax import lax
from jax.experimental import pallas as pl
from jax.experimental.pallas import tpu as pltpu
from jax.sharding import PartitionSpec as P

MESH = pl.DeviceIdType.MESH
F32 = jnp.float32
BF16 = jnp.bfloat16
X, Y, Z = 0, 1, 2
NP = 8
CAP = 24
PAIR = 2 * CAP
SUB = (0, -1, 1, 2)

ORDERS = (
    (Y, X, Z),
    (Z, Y, X),
    (Z, X, Y),
    (Y, X, Z),
    (X, Y, Z),
    (Z, Y, X),
    (X, Z, Y),
    (Z, X, Y),
)
BACK = (
    (Y, X, Z),
    (X, Y, Z),
    (X, Z, Y),
    (Z, Y, X),
    (Y, X, Z),
    (Z, Y, X),
    (Z, X, Y),
    (Z, X, Y),
)
THERE = ((8, 6, 1), (6, 11, 2), (0, 1, 8), (9, 9, 7), (8, 4, 13), (3, 4, 10), (5, 0, 12), (7, 8, 6))
HOME = ((23, 18, 24), (27, 21, 23), (22, 23, 17), (25, 22, 23), (28, 15, 16), (26, 19, 25), (27, 26, 14), (20, 14, 15))
FIRST = (3, 7, 4, 2, 6, 0, 1, 5)
SECOND = (0, 3, 2, 1, 4, 7, 6, 5)
BACKLOG = 3.0

COST = dict(SEL=0.76, SLOT=0.35, GU=1.9, HID=1.0, DN=1.45, CB=0.88, CBS=0.45, META=0.3, SB=0.12, ADD=0.12)


def tasks_of(orders, back):
    t = {}

    def add(name, group, cost, after=(), needs=(), sends=()):
        t[name] = (group, cost, tuple(after), tuple(needs), tuple(sends))

    def size_of(axis, ph):
        return 16384 if ph == 0 else 49152 if (ph == 2 and axis == Y) else 65536

    def phase(tag, axis, j, ph, s, per, before, second=(), up=(), down=(), last=()):
        k = (j, ph, s)
        size = size_of(axis, ph)
        v = 0.04 + per * size / 262144
        s0, s1, fp, fm = (tag + "S0",) + k, (tag + "S1",) + k, (tag + "F+",) + k, (tag + "F-",) + k
        group = (tag, j, ph, s if tag == "A" else 3 - s)
        add(s0, group + (0,), 0.04, before, (), [(axis, 1, size, ("a+", tag) + k), (axis, -1, size, ("a-", tag) + k)])
        add(s1, group + (1,), 0.04, [s0, *second], (), [(axis, 1, size, ("b+", tag) + k), (axis, -1, size, ("b-", tag) + k)])
        add(fp, group + (-1,), v, [s1, *up], [("a+", tag) + k], [(axis, 1, size, ("c+", tag) + k)])
        add(fm, group + (-1,), v, [s1, *down], [("a-", tag) + k], [(axis, -1, size, ("c-", tag) + k)])
        g = group + (-2,)
        if tag == "A" and ph == 1:
            add(("AB+",) + k, g, 0.02, [fp], [("b+", tag) + k])
            add(("AB-",) + k, g, 0.02, [fm], [("b-", tag) + k])
            add(("AD",) + k, g, 0.02, [("AB+",) + k, ("AB-",) + k], [("c+", tag) + k, ("c-", tag) + k])
        else:
            add((tag + "D",) + k, g, 2 * v if per else 0.02, [fp, fm, *last], [(n, tag) + k for n in ("b+", "b-", "c+", "c-")])

    sb = [("SB", q) for q in range(NP)]
    for j in range(NP):
        order, slot = orders[j], orders[j][2] == Y
        phase("A", order[0], j, 0, 0, 0, [])
        phase("A", order[1], j, 1, 0, 0, [("AD", j, 0, 0)])
        if slot:
            add(("SEL", j), ("SLOT", j), COST["SLOT"], [("AD", j, 1, 0)] + sb)
        for s in range(4):
            before = [("SEL", j)] if slot else [(("AD", j, 0, 0), ("AB+", j, 1, 0), ("AB-", j, 1, 0), ("AD", j, 1, 0))[s]]
            phase("A", order[2], j, 2, s, 0, before)
        here = [("AD", j, 2, s) for s in range(4)]
        if not slot:
            add(("SEL", j), ("SEL", j), COST["SEL"], here + sb)
        add(("GU", j), ("GU", j), COST["GU"], [("SEL", j)] + here, [("pw", j)])
        add(("DN", j), ("DN", j), COST["DN"], [("HID",)], [("pd",)])
        order, add_us = back[j], COST["ADD"]
        d = [("RD", j, 2, i) for i in range(4)]
        if slot:
            add(("CB", j), ("CBS", j), COST["CBS"], d)
        else:
            add(("CB", j), ("CB", j), COST["CB"], [("DN", j)])
        for s in (3, 2, 1, 0):
            phase("R", order[2], j, 2, s, add_us, [("DN" if slot else "CB", j)])
        if slot:
            phase("R", order[1], j, 1, 0, add_us, [("CB", j)])
        else:
            phase("R", order[1], j, 1, 0, add_us, [d[3]], [d[1], d[2]], [d[2]], [d[1]], [d[0]])
        phase("R", order[0], j, 0, 0, add_us, [("RD", j, 1, 0)])
    add(("META",), ("META",), COST["META"], (), [("meta",)])
    for q in range(NP):
        add(("SB", q), ("SB", q), COST["SB"], [("META",)])
    add(("HID",), ("HID",), COST["HID"], [("GU", j) for j in range(NP)])
    return t


def priority(there, home, first, second):
    def rank(g):
        if g[0] == "A":
            return (0, -9 if g[4] == -2 else there[g[1]][g[2]], g[3], g[4])
        if g[0] == "R":
            return (0, home[g[1]][g[2]], g[3], g[4])
        if g[0] == "CBS":
            return (0, home[g[1]][2], 9, 0)
        if g[0] in ("META", "SB", "SLOT"):
            return (1, 0, 0, 0)
        if g[0] in ("SEL", "GU"):
            return (2, first[g[1]], g[0] == "GU", 0)
        if g[0] == "HID":
            return (2, 50, 0, 0)
        return (2, 100 + second[g[1]], g[0] == "CB", 0)

    return rank


def plan(t, rank, backlog, trace=None):
    rate, lat = 46.6e3, 2.4
    arrive = {("meta",): 5.0, ("pd",): 54.0}
    for j in range(NP):
        arrive[("pw", j)] = 8.5 + 4.5 * j
    left = {k: len(v[2]) for k, v in t.items()}
    after = {}
    for k, v in t.items():
        for d in v[2]:
            after.setdefault(d, []).append(k)
    avail = [k for k, c in left.items() if c == 0]
    free, now, out = {}, 0.0, []
    while avail:
        best, later = None, 1e9
        for k in avail:
            group, cost, _, needs, sends = t[k]
            when = 0.0
            for n in needs:
                when = max(when, arrive.get(n, 1e9))
            if not needs:
                for a, d, _, _ in sends:
                    when = max(when, free.get((a, d), 0.0) - backlog)
            if when <= now + 1e-9:
                p = rank(group)
                if best is None or (p, k) < best:
                    best = (p, k)
            elif when < later:
                later = when
        if best is None:
            now = later
            continue
        k = best[1]
        avail.remove(k)
        _, cost, _, _, sends = t[k]
        now += cost
        for a, d, size, tag in sends:
            begin = max(now, free.get((a, d), 0.0))
            free[(a, d)] = begin + size / rate
            arrive[tag] = begin + size / rate + lat
        out.append(k)
        if trace is not None:
            trace.append((round(now, 1), k))
        for q in after.get(k, ()):
            left[q] -= 1
            if left[q] == 0:
                avail.append(q)
    return out, now


def schedule():
    trace = []
    plan(tasks_of(ORDERS, BACK), priority(THERE, HOME, FIRST, SECOND), BACKLOG, trace)
    gu = [k[1] for _, k in trace if k[0] == "GU"]
    dn = [k[1] for _, k in trace if k[0] == "DN"]
    out, early = [], [(14.0, gu[0]), (19.0, gu[1])]
    for when, k in trace:
        while early and when >= early[0][0]:
            out.append(("LW", early.pop(0)[1]))
        out.append(k)
        if k[0] == "GU":
            i = gu.index(k[1]) + 2
            out += [("LW", gu[i])] if i < NP else [("DW", dn[i - NP])]
        if k[0] == "DN" and dn.index(k[1]) + 2 < NP:
            out.append(("DW", dn[dn.index(k[1]) + 2]))
    return out, gu, dn


SCHEDULE, GU_ORDER, DN_ORDER = schedule()
SLOTTED = [j for j in range(NP) if ORDERS[j][2] == Y]
PLAIN = [j for j in range(NP) if ORDERS[j][2] != Y]


def unit(ph, s):
    return ph + s


def half_shape(j, order, ph):
    if j in SLOTTED and ph == 2:
        return (192, 128)
    full = order[:min(ph, 1)]
    return (4 if X in full else 1, 4 if Z in full else 1, 64, 512 if Y in full else 128)


def kernel(tok, meta, gw, uw, dw, out, pw, pd, t_ref, ts_ref, xs_ref, ys_ref, w_ref, d_ref, x_ref, acc, hid, y_ref,
           s_ref, st_ref, ps, rk, pr, mb, ga, gb, gc, gs, ra, rc, rs, tok_sem, meta_send, meta_recv, meta_own,
           pw_send, pw_recv, pd_send, pd_recv, w_sem, d_sem, *rb):
    ep = lax.axis_index("ep")
    y = lax.axis_index("etp")
    x, z, core = ep // 8, (ep // 2) % 4, ep % 2
    own = (x, y, z)

    def at(axis, delta):
        c = [x, y, z]
        c[axis] = (c[axis] + delta + 4) % 4
        return {"ep": c[X] * 8 + c[Z] * 2 + core, "etp": c[Y]}

    partner = {"ep": x * 8 + z * 2 + (1 - core), "etp": y}
    plane = [
        {"ep": ((x + dx) % 4) * 8 + ((z + dz) % 4) * 2 + core, "etp": y}
        for dx in range(4) for dz in range(4) if dx or dz
    ]

    def lanes(i, n=1):
        return pl.ds(pl.multiple_of(i * 128, 128), 128 * n)

    own_tok = []
    for j in range(NP):
        dst = ts_ref.at[SLOTTED.index(j), x, z] if j in SLOTTED else t_ref.at[PLAIN.index(j), x, z, :, lanes(y)]
        own_tok.append(pltpu.make_async_copy(tok.at[:, pl.ds(j * 128, 128)], dst, tok_sem.at[j]))
    for c in own_tok:
        c.start()
    g = x * 4 + z
    own_meta = pltpu.make_async_copy(meta, mb.at[g], meta_own)
    own_meta.start()

    barrier = pltpu.get_barrier_semaphore()
    greet = plane + [at(Y, 1), at(Y, -1), partner]
    for d in greet:
        pl.semaphore_signal(barrier, inc=1, device_id=d, device_id_type=MESH)
    pl.semaphore_wait(barrier, len(greet))

    def remote(src, dst, ssem, rsem, dev):
        pltpu.make_async_remote_copy(src_ref=src, dst_ref=dst, send_sem=ssem, recv_sem=rsem,
                                     device_id=dev, device_id_type=MESH).start()

    def wait(ref, sem):
        pltpu.make_async_copy(ref, ref, sem).wait()

    def place(axis, delta):
        return (own[axis] + delta + 4) % 4

    def spot(order, ph, pos, sub):
        p = list(own)
        if ph >= 1:
            p[order[0]] = None
        if ph == 2:
            p[order[1]] = place(order[1], SUB[sub])
        p[order[ph]] = pos
        return p

    def slab(order, j, ph, sub, pos, half=None, many=1):
        if j in SLOTTED and ph == 2:
            rows = pl.ds(0, 384) if half is None else pl.ds(192 * half, 192)
            return xs_ref.at[SLOTTED.index(j), sub, rows, lanes(pos, many)]
        p, a = spot(order, ph, pos, sub), order[ph]
        rows = pl.ds(0, 128) if half is None else pl.ds(64 * half, 64)
        ix, iz = (pl.ds(0, 4) if p[i] is None else pl.ds(p[i], many if i == a else 1) for i in (X, Z))
        if j in SLOTTED:
            return ts_ref.at[SLOTTED.index(j), ix, iz, rows, :]
        cols = pl.ds(0, 512) if p[Y] is None else lanes(p[Y], many if a == Y else 1)
        return t_ref.at[PLAIN.index(j), ix, iz, rows, cols]

    def run_as(j, ph, s, first):
        if ph == 0 and first:
            own_tok[j].wait()
        o = ORDERS[j]
        a, u = o[ph], unit(ph, s)
        p = own[a]
        for half, sign in ((0, 1), (1, -1)) if first else ((1, 1), (0, -1)):
            if first:
                sem = ga.at[j, u, half]
            elif ph == 1:
                sem = gb.at[j, half]
            else:
                sem = gc.at[j, u]
            h = slab(o, j, ph, s, p, half)
            remote(h, h, gs.at[j, u], sem, at(a, sign))

    def run_af(j, ph, s, sign):
        o, u = ORDERS[j], unit(ph, s)
        half = 0 if sign > 0 else 1
        ref = slab(o, j, ph, s, place(o[ph], -sign), half)
        wait(ref, ga.at[j, u, half])
        remote(ref, ref, gs.at[j, u], gc.at[j, u], at(o[ph], sign))

    def run_ab(j, ph, s, sign):
        half = 1 if sign > 0 else 0
        wait(slab(ORDERS[j], j, ph, s, place(ORDERS[j][ph], -sign), half), gb.at[j, half])

    def run_ad(j, ph, s):
        wait(slab(ORDERS[j], j, ph, s, 0, None, 1 if ph == 1 else 2), gc.at[j, unit(ph, s)])

    def run_lw(j):
        wait(pw.at[j], pw_recv.at[j])
        slot = GU_ORDER.index(j) % 2
        for e in range(2):
            for m, src in ((0, gw), (1, uw)):
                s = pw.at[j, m] if e else src.at[:, :, j]
                pltpu.make_async_copy(s, w_ref.at[slot, pl.ds(2 * e, 2), :, :, pl.ds(m * 384, 384)], w_sem.at[slot]).start()

    def run_dw(j):
        if j == DN_ORDER[0]:
            wait(pd, pd_recv)
        slot = DN_ORDER.index(j) % 2
        for e, src in ((0, dw), (1, pd)):
            for k in range(4):
                pltpu.make_async_copy(
                    src.at[:, :, pl.ds(k * 1024 + j * 128, 128)],
                    d_ref.at[slot, pl.ds(2 * e, 2), :, pl.ds(k * 128, 128)], d_sem.at[slot]).start()

    def run_meta():
        own_meta.wait()
        wait(mb.at[pl.ds(0, 15)], meta_recv)
        ids = mb[:, 0:8, :]
        probs = mb[:, 8:16, :]
        chip = (x * 4 + z) * 4
        rows, prows = [], []
        for e in (chip + 2 * core, chip + 2 * core + 1, chip + 2 * (1 - core), chip + 2 * (1 - core) + 1):
            hit = ids == e.astype(F32)
            rows.append(jnp.sum(jnp.where(hit, 1.0, 0.0), axis=1))
            prows.append(jnp.sum(jnp.where(hit, probs, 0.0), axis=1))
        ind = jnp.concatenate(rows, axis=0)
        pr[...] = jnp.concatenate(prows, axis=0)
        upper = (lax.broadcasted_iota(jnp.int32, (128, 128), 0) < lax.broadcasted_iota(jnp.int32, (128, 128), 1))
        rank = jnp.dot(ind.astype(BF16), jnp.where(upper, 1.0, 0.0).astype(BF16), preferred_element_type=F32)
        odd = (lax.broadcasted_iota(jnp.int32, (64, 128), 0) % 2).astype(F32) * float(CAP)
        rk[...] = jnp.where(ind > 0.5, rank + odd, -1.0)

    def run_sb(q):
        row = lax.broadcasted_iota(jnp.int32, (PAIR, 128), 0).astype(F32)
        blocks = []
        for e in range(4):
            i = e * 16 + 2 * q
            left = jnp.where(row == rk[i:i + 1, :], 1.0, 0.0)
            right = jnp.where(row == rk[i + 1:i + 2, :], 1.0, 0.0)
            weight = jnp.sum(left * pr[i:i + 1, :] + right * pr[i + 1:i + 2, :], axis=1, keepdims=True)
            ps[e, q * PAIR:(q + 1) * PAIR, :] = jnp.broadcast_to(0.5 * weight, (PAIR, 128))
            blocks.append(jnp.concatenate([left, right], axis=1))
        blocks.append(jnp.zeros((256 - 4 * PAIR, 256), F32))
        full = jnp.concatenate(blocks, axis=0)
        s_ref[q] = full[:4 * PAIR].astype(BF16)
        st_ref[q] = full.T.astype(BF16)
        y_ref[q, 4 * PAIR:, :] = jnp.zeros((256 - 4 * PAIR, 512), BF16)
        for i in range(len(SLOTTED)):
            ys_ref[i, q, 4 * PAIR:, :] = jnp.zeros((256 - 4 * PAIR, 128), BF16)

    def run_sel(j):
        slotted = j in SLOTTED

        def step(i, carry):
            for k in range(4):
                q = 4 * i + k
                gx, gz = 2 * i + k // 2, slice((k % 2) * 2, (k % 2) * 2 + 2)
                if slotted:
                    t = ts_ref[SLOTTED.index(j), gx, gz].reshape(256, 128)
                else:
                    t = t_ref[PLAIN.index(j), gx, gz].reshape(256, 512)
                r = jnp.dot(s_ref[q], t, preferred_element_type=F32).astype(BF16)
                for e in range(4):
                    rows = pl.ds(pl.multiple_of(q * PAIR, 16), PAIR)
                    if slotted:
                        xs_ref[SLOTTED.index(j), e, rows, lanes(y)] = r[e * PAIR:(e + 1) * PAIR]
                    else:
                        x_ref[e, rows, :] = r[e * PAIR:(e + 1) * PAIR]
            return carry

        lax.fori_loop(0, 2, step, 0)

    def run_gu(j):
        slot = GU_ORDER.index(j) % 2
        wait(w_ref.at[slot], w_sem.at[slot])

        def step(e, carry):
            rows = xs_ref[SLOTTED.index(j), e] if j in SLOTTED else x_ref[e]
            for n in range(3):
                w = w_ref[slot, e, :, :, n * 256:(n + 1) * 256].reshape(512, 256)
                r = jnp.dot(rows, w, preferred_element_type=F32)
                if j == GU_ORDER[0]:
                    acc[e, :, n * 256:(n + 1) * 256] = r
                else:
                    acc[e, :, n * 256:(n + 1) * 256] += r
            return carry

        lax.fori_loop(0, 4, step, 0)

    def run_hid():
        def step(i, carry):
            e, k = i // 4, i % 4
            rows = pl.ds(pl.multiple_of(k * 96, 16), 96)
            w = ps[e, rows, :]
            for n in range(3):
                gate, up = acc[e, rows, n * 128:(n + 1) * 128], acc[e, rows, 384 + n * 128:384 + (n + 1) * 128]
                h = (gate * up * w) * (1.0 + jnp.tanh(0.5 * gate))
                hid[e, rows, n * 128:(n + 1) * 128] = h.astype(BF16)
            return carry

        lax.fori_loop(0, 16, step, 0)

    def run_dn(j):
        slot = DN_ORDER.index(j) % 2
        wait(d_ref.at[slot], d_sem.at[slot])
        slotted = j in SLOTTED
        if slotted:
            for s in range(4):
                wait(slab(ORDERS[j], j, 2, s, 0, None, 3), gs.at[j, unit(2, s)])

        def step(e, carry):
            r = jnp.dot(hid[e], d_ref[slot, e], preferred_element_type=F32).astype(BF16)
            if slotted:
                xs_ref[SLOTTED.index(j), e] = r
            else:
                for q in range(NP):
                    y_ref[q, pl.ds(pl.multiple_of(e * PAIR, 16), PAIR), :] = r[q * PAIR:(q + 1) * PAIR]
            return carry

        lax.fori_loop(0, 4, step, 0)

    def run_cb(j):
        slotted = j in SLOTTED
        for ph, s in ((0, 0), (1, 0)) + (() if slotted else tuple((2, s) for s in range(4))):
            wait(slab(ORDERS[j], j, ph, s, 0, None, 3), gs.at[j, unit(ph, s)])

        def step(i, carry):
            for k in range(4):
                q = 4 * i + k
                gx, gz = 2 * i + k // 2, slice((k % 2) * 2, (k % 2) * 2 + 2)
                rows = ys_ref[SLOTTED.index(j), q] if slotted else y_ref[q]
                r = jnp.dot(st_ref[q], rows, preferred_element_type=F32).astype(BF16)
                if slotted:
                    ts_ref[SLOTTED.index(j), gx, gz] = r.reshape(2, 128, 128)
                else:
                    t_ref[PLAIN.index(j), gx, gz] = r.reshape(2, 128, 512)
            return carry

        lax.fori_loop(0, 2, step, 0)

    def buf(j, ph, s):
        return rb[3 * j + ph].at[s]

    def run_rs(j, ph, s, first):
        o = BACK[j]
        a, u = o[ph], unit(ph, s)
        b = buf(j, ph, s)
        for half, sign in ((0, 1), (1, -1)) if first else ((1, 1), (0, -1)):
            pos = place(a, 2 if first else sign)
            sem = ra.at[j, u, half] if first else rc.at[j, u]
            remote(slab(o, j, ph, s, pos, half), b.at[half if first else 3 - half], rs.at[j, u], sem, at(a, sign))

    def add_into(j, ph, s, pos, half, parts, final):
        b, o = rb[3 * j + ph], BACK[j]
        if j in SLOTTED and ph == 2:
            i = SLOTTED.index(j)
            v = xs_ref[i, s, pl.ds(192 * half, 192), lanes(pos)].astype(F32)
            for k in parts:
                v = v + b[s, k].astype(F32)
            v = v.astype(BF16)
            if final:
                for q in range(4):
                    ys_ref[i, 4 * half + q, s * PAIR:(s + 1) * PAIR, :] = v[q * PAIR:(q + 1) * PAIR]
            else:
                xs_ref[i, s, pl.ds(192 * half, 192), lanes(pos)] = v
            return
        nx, nz, _, cols = half_shape(j, o, ph)
        p = spot(o, ph, pos, s)
        rows = pl.ds(64 * half, 64)

        def step(i, carry):
            ix, iz = i // nz, i % nz
            gx, gz = ix if p[X] is None else p[X], iz if p[Z] is None else p[Z]
            if j in SLOTTED:
                ref, where = ts_ref, (SLOTTED.index(j), gx, gz, rows, slice(None))
            else:
                ref = t_ref
                where = (PLAIN.index(j), gx, gz, rows, slice(None) if p[Y] is None else lanes(p[Y]))
            v = ref[where].astype(F32)
            for k in parts:
                v = v + b[s, k, ix, iz].astype(F32)
            v = v.astype(BF16)
            if final and ph == 0:
                out[rows, j * 128:(j + 1) * 128] = v
            else:
                ref[where] = v
            return carry

        if nx * nz == 1:
            step(0, 0)
        else:
            lax.fori_loop(0, nx * nz, step, 0)

    def run_rf(j, ph, s, sign):
        o, u, b = BACK[j], unit(ph, s), buf(j, ph, s)
        half = 0 if sign > 0 else 1
        wait(b.at[half], ra.at[j, u, half])
        pos = place(o[ph], sign)
        add_into(j, ph, s, pos, half, (half,), False)
        remote(slab(o, j, ph, s, pos, half), b.at[4 + half], rs.at[j, u], rc.at[j, u], at(o[ph], sign))

    def run_rd(j, ph, s):
        wait(buf(j, ph, s).at[pl.ds(2, 4)], rc.at[j, unit(ph, s)])
        p = own[BACK[j][ph]]
        add_into(j, ph, s, p, 0, (3, 4), True)
        add_into(j, ph, s, p, 1, (2, 5), True)

    started = 0
    while SCHEDULE[started][0] in ("AS0", "AS1"):
        k = SCHEDULE[started]
        run_as(*k[1:], k[0] == "AS0")
        started += 1
    for d in plane:
        remote(meta, mb.at[g], meta_send, meta_recv, d)
    for j in GU_ORDER:
        remote(gw.at[:, :, j], pw.at[j, 0], pw_send, pw_recv.at[j], partner)
        remote(uw.at[:, :, j], pw.at[j, 1], pw_send, pw_recv.at[j], partner)
    remote(dw, pd, pd_send, pd_recv, partner)

    runs = {
        "AS0": lambda *k: run_as(*k, True), "AS1": lambda *k: run_as(*k, False),
        "AF+": lambda *k: run_af(*k, 1), "AF-": lambda *k: run_af(*k, -1),
        "AB+": lambda *k: run_ab(*k, 1), "AB-": lambda *k: run_ab(*k, -1), "AD": run_ad,
        "LW": run_lw, "DW": run_dw, "SEL": run_sel, "GU": run_gu, "DN": run_dn, "CB": run_cb,
        "RS0": lambda *k: run_rs(*k, True), "RS1": lambda *k: run_rs(*k, False),
        "RF+": lambda *k: run_rf(*k, 1), "RF-": lambda *k: run_rf(*k, -1), "RD": run_rd,
        "META": run_meta, "SB": run_sb, "HID": run_hid,
    }
    for task in SCHEDULE[started:]:
        runs[task[0]](*task[1:])

    for j in range(NP):
        for ph in range(3):
            for s in range(4 if ph == 2 else 1):
                wait(slab(BACK[j], j, ph, s, 0, None, 3), rs.at[j, unit(ph, s)])
    wait(mb.at[pl.ds(0, 15)], meta_send)
    wait(pw, pw_send)
    wait(pd, pd_send)


def body(tokens, expert_ids, gate_prob, gate_weight, up_weight, down_weight):
    meta = jnp.concatenate([expert_ids.T.astype(F32), gate_prob.T], axis=0)
    gw = gate_weight.reshape(2, 4, NP, 128, 384)
    uw = up_weight.reshape(2, 4, NP, 128, 384)
    hbm = pl.BlockSpec(memory_space=pl.ANY)
    dma = pltpu.SemaphoreType.DMA
    ns = len(SLOTTED)
    scratch = [
        pltpu.VMEM((NP - ns, 4, 4, 128, 512), BF16),
        pltpu.VMEM((ns, 4, 4, 128, 128), BF16),
        pltpu.VMEM((ns, 4, 384, 512), BF16),
        pltpu.VMEM((ns, 8, 256, 128), BF16),
        pltpu.VMEM((2, 4, 4, 128, 768), BF16),
        pltpu.VMEM((2, 4, 384, 512), BF16),
        pltpu.VMEM((4, 384, 512), BF16),
        pltpu.VMEM((4, 384, 768), F32),
        pltpu.VMEM((4, 384, 384), BF16),
        pltpu.VMEM((8, 256, 512), BF16),
        pltpu.VMEM((8, 4 * PAIR, 256), BF16),
        pltpu.VMEM((8, 256, 256), BF16),
        pltpu.VMEM((4, 384, 128), F32),
        pltpu.VMEM((64, 128), F32),
        pltpu.VMEM((64, 128), F32),
        pltpu.VMEM((16, 16, 128), F32),
        dma((NP, 6, 2)), dma((NP, 2)), dma((NP, 6)), dma((NP, 6)),
        dma((NP, 6, 2)), dma((NP, 6)), dma((NP, 6)),
        dma((NP,)), dma, dma, dma, dma, dma((NP,)), dma, dma, dma((2,)), dma((2,)),
    ] + [
        pltpu.VMEM((4 if ph == 2 else 1, 6) + half_shape(j, BACK[j], ph), BF16)
        for j in range(NP) for ph in range(3)
    ]
    return pl.pallas_call(
        kernel,
        name="moe",
        out_shape=(
            jax.ShapeDtypeStruct((128, 1024), BF16),
            jax.ShapeDtypeStruct((NP, 2, 2, 4, 128, 384), BF16),
            jax.ShapeDtypeStruct((2, 384, 4096), BF16),
        ),
        in_specs=[hbm] * 5,
        out_specs=(pl.BlockSpec(memory_space=pltpu.VMEM), hbm, hbm),
        scratch_shapes=scratch,
        compiler_params=pltpu.CompilerParams(collective_id=0, has_side_effects=True, vmem_limit_bytes=67043328),
    )(tokens, meta, gw, uw, down_weight)[0]


def solution(mesh):
    in_specs = (
        P("ep", "etp"),
        P("ep", None),
        P("ep", None),
        P("ep", None, "etp"),
        P("ep", None, "etp"),
        P("ep", "etp", None),
    )
    return jax.shard_map(body, mesh=mesh, in_specs=in_specs, out_specs=P("ep", "etp"), check_vma=False)
```

time: 188 us -> 150 us (0.80)
  Pallas kernels: 184 us -> 146 us
    pallas_call x1, Pallas kernels: 184 us -> 146 us  [body(): pl.pallas_call(kernel, name='moe', out_shape=(jax.ShapeDtypeStruct((128,...]
where the time goes in v2:
time: 150 us
  Pallas kernels  146 us (97%)
  other arithmetic  1.97 us (1%)
  local copies, waits for them, and re-layouts  1.67 us (1%)
    pallas_call x1, Pallas kernels, body(): pl.pallas_call(kernel, name='moe', out_shape=(jax.ShapeDtypeStruct((128,...  146 us

profile of v2, /device:TPU:0, one launch (start us, length us, event | category | flops | bytes accessed | tf_op | source)
XLA Modules:
  0.0 149.6 jit_solution(14576530780223940991)
XLA Ops:
  0.0 0.7 convert_bitcast_fusion
  0.7 1.3 pad_maximum_fusion.meta
  2.0 145.9 %moe.1 = (bf16[128,1024]{1,0:T(8,128)(2,1)}, bf16[8,2,2,4,128,384]{5,4,3,2,1,0:T(8,128)(2,1)}, bf16[2,384,4096]{2,1,0:T(8,128)(2,1)}) custom-call(bf16[128,1024]{1,0:T(8,128)(2,1)} %tok.1, f32[16,128]{1,0:T(8,128)} %pad_maximum_fusion.meta, bf16[2,4,8,128,384]{4,3,2,1,0:T(8,128)(2,1)} %bitcast.5, bf16[2,4,8,128,384]{4,3,2,1,0:T(8,128)(2,1)} %bitcast.6, ...), custom_call_target="tpu_custom_call" | custom-call | tf_op jit(solution)/shard_map/moe/pallas_call | solution.py:584
  147.9 1.7 %copy.8 = bf16[128,1024]{1,0:T(8,128)(2,1)} copy(bf16[128,1024]{1,0:T(8,128)(2,1)} %get-tuple-element.6) | data formatting | bytes 524288

commit v3 on v2

--- a/solution.py
+++ b/solution.py
@@ -15,42 +15,43 @@
 SUB = (0, -1, 1, 2)
 
 ORDERS = (
+    (Z, Y, X),
+    (Z, X, Y),
+    (X, Y, Z),
+    (Z, X, Y),
     (Y, X, Z),
     (Z, Y, X),
     (Z, X, Y),
-    (Y, X, Z),
     (X, Y, Z),
-    (Z, Y, X),
-    (X, Z, Y),
-    (Z, X, Y),
 )
 BACK = (
-    (Y, X, Z),
     (X, Y, Z),
-    (X, Z, Y),
-    (Z, Y, X),
+    (Z, X, Y),
+    (X, Y, Z),
+    (Z, X, Y),
     (Y, X, Z),
     (Z, Y, X),
     (Z, X, Y),
-    (Z, X, Y),
+    (Z, Y, X),
 )
-THERE = ((8, 6, 1), (6, 11, 2), (0, 1, 8), (9, 9, 7), (8, 4, 13), (3, 4, 10), (5, 0, 12), (7, 8, 6))
-HOME = ((23, 18, 24), (27, 21, 23), (22, 23, 17), (25, 22, 23), (28, 15, 16), (26, 19, 25), (27, 26, 14), (20, 14, 15))
-FIRST = (3, 7, 4, 2, 6, 0, 1, 5)
-SECOND = (0, 3, 2, 1, 4, 7, 6, 5)
-BACKLOG = 3.0
-
+THERE = ((2, 9, 11), (5, 2, 0), (10, 4, 2), (10, 3, 2), (10, 8, 2), (2, 3, 12), (10, 11, 3), (1, 9, 6))
+HOME = ((3, 11, 11), (9, 4, 10), (5, 11, 7), (10, 3, 10), (1, 8, 11), (13, 11, 1), (7, 11, 10), (13, 11, 7))
+FIRST = (0, 1, 2, 3, 4, 5, 6, 7)
+SECOND = (2, 6, 5, 4, 7, 1, 3, 0)
+BACKLOG = 2.0
+
+SPLIT = (1, 4, 4)
 COST = dict(SEL=0.76, SLOT=0.35, GU=1.9, HID=1.0, DN=1.45, CB=0.88, CBS=0.45, META=0.3, SB=0.12, ADD=0.12)
 
 
-def tasks_of(orders, back):
+def tasks_of(orders, back, first, second):
     t = {}
 
     def add(name, group, cost, after=(), needs=(), sends=()):
         t[name] = (group, cost, tuple(after), tuple(needs), tuple(sends))
 
     def size_of(axis, ph):
-        return 16384 if ph == 0 else 49152 if (ph == 2 and axis == Y) else 65536
+        return 16384 if ph < 2 else 49152 if axis == Y else 65536
 
     def phase(tag, axis, j, ph, s, per, before, second=(), up=(), down=(), last=()):
         k = (j, ph, s)
@@ -63,45 +64,93 @@
         add(fp, group + (-1,), v, [s1, *up], [("a+", tag) + k], [(axis, 1, size, ("c+", tag) + k)])
         add(fm, group + (-1,), v, [s1, *down], [("a-", tag) + k], [(axis, -1, size, ("c-", tag) + k)])
         g = group + (-2,)
-        if tag == "A" and ph == 1:
+        if tag == "A" and ph < 2:
             add(("AB+",) + k, g, 0.02, [fp], [("b+", tag) + k])
             add(("AB-",) + k, g, 0.02, [fm], [("b-", tag) + k])
             add(("AD",) + k, g, 0.02, [("AB+",) + k, ("AB-",) + k], [("c+", tag) + k, ("c-", tag) + k])
         else:
             add((tag + "D",) + k, g, 2 * v if per else 0.02, [fp, fm, *last], [(n, tag) + k for n in ("b+", "b-", "c+", "c-")])
 
+    def every(kind, j, ph):
+        return [(kind, j, ph, s) for s in range(SPLIT[ph])]
+
+    def parts(split):
+        return range(4) if split else (None,)
+
+    def share(kind, e):
+        return COST[kind] if e is None else COST[kind] / 4
+
+    def gu_end(j):
+        return ("GU", j, 3 if j == first[-1] else None)
+
+    def dn_end(j):
+        return ("DN", j, 3 if second.index(j) < 2 else None)
+
     sb = [("SB", q) for q in range(NP)]
+    plain = [j for j in first if orders[j][2] != Y]
+    back_plain = [j for j in second if orders[j][2] != Y]
     for j in range(NP):
         order, slot = orders[j], orders[j][2] == Y
-        phase("A", order[0], j, 0, 0, 0, [])
-        phase("A", order[1], j, 1, 0, 0, [("AD", j, 0, 0)])
+        for ph in range(3):
+            for s in range(SPLIT[ph]):
+                if ph == 0:
+                    before = []
+                elif ph == 2 and slot:
+                    before = [("SEL", j)]
+                elif ph == 2 and s == 0:
+                    before = every("AD", j, 0)
+                elif SPLIT[ph] == 1:
+                    before = every("AD", j, ph - 1)
+                else:
+                    before = ([], every("AB+", j, ph - 1), every("AB-", j, ph - 1), every("AD", j, ph - 1))[s]
+                phase("A", order[ph], j, ph, s, 0, before)
+        at = first.index(j)
+        turn = [gu_end(first[at - 1])] if at else []
         if slot:
-            add(("SEL", j), ("SLOT", j), COST["SLOT"], [("AD", j, 1, 0)] + sb)
-        for s in range(4):
-            before = [("SEL", j)] if slot else [(("AD", j, 0, 0), ("AB+", j, 1, 0), ("AB-", j, 1, 0), ("AD", j, 1, 0))[s]]
-            phase("A", order[2], j, 2, s, 0, before)
-        here = [("AD", j, 2, s) for s in range(4)]
-        if not slot:
-            add(("SEL", j), ("SEL", j), COST["SEL"], here + sb)
-        add(("GU", j), ("GU", j), COST["GU"], [("SEL", j)] + here, [("pw", j)])
-        add(("DN", j), ("DN", j), COST["DN"], [("HID",)], [("pd",)])
+            add(("SEL", j), ("SLOT", j), COST["SLOT"], every("AD", j, 1) + sb)
+        else:
+            i = plain.index(j)
+            add(("SEL", j), ("SEL", j), COST["SEL"], every("AD", j, 2) + sb + ([gu_end(plain[i - 2])] if i > 1 else []))
+        for e in parts(j == first[-1]):
+            here = every("AD", j, 2) if e is None else [("AD", j, 2, e)]
+            prev = [("GU", j, e - 1)] if e else turn
+            add(("GU", j, e), ("GU", j, e or 0), share("GU", e), [("SEL", j)] + (here if slot else []) + prev, [("pw", at)])
+        at = second.index(j)
+        i = 0 if slot else back_plain.index(j)
+        for e in parts(at < 2):
+            prev = [("DN", j, e - 1)] if e else []
+            if at == 1:
+                prev.append(("DN", second[0], e))
+            if at > 1:
+                prev += [dn_end(second[at - 1]), dn_end(second[at - 2])]
+            if not slot and i > 1:
+                prev.append(("CB", back_plain[i - 2]))
+            add(("DN", j, e), ("DN", j, e or 0), share("DN", e), [("HID", 3 if e is None else e)] + prev, [("pd",)])
         order, add_us = back[j], COST["ADD"]
-        d = [("RD", j, 2, i) for i in range(4)]
         if slot:
-            add(("CB", j), ("CBS", j), COST["CBS"], d)
+            add(("CB", j), ("CBS", j), COST["CBS"], every("RD", j, 2))
         else:
-            add(("CB", j), ("CB", j), COST["CB"], [("DN", j)])
-        for s in (3, 2, 1, 0):
-            phase("R", order[2], j, 2, s, add_us, [("DN" if slot else "CB", j)])
-        if slot:
-            phase("R", order[1], j, 1, 0, add_us, [("CB", j)])
-        else:
-            phase("R", order[1], j, 1, 0, add_us, [d[3]], [d[1], d[2]], [d[2]], [d[1]], [d[0]])
-        phase("R", order[0], j, 0, 0, add_us, [("RD", j, 1, 0)])
-    add(("META",), ("META",), COST["META"], (), [("meta",)])
+            add(("CB", j), ("CB", j), COST["CB"], [dn_end(j)])
+        for ph in (2, 1, 0):
+            for s in range(SPLIT[ph] - 1, -1, -1):
+                if ph == 2:
+                    phase("R", order[2], j, 2, s, add_us, [(("DN", j, s) if at < 2 else dn_end(j)) if slot else ("CB", j)])
+                elif ph == 1 and slot:
+                    phase("R", order[1], j, 1, s, add_us, [("CB", j)])
+                elif SPLIT[ph + 1] == 1:
+                    phase("R", order[ph], j, ph, s, add_us, [("RD", j, ph + 1, 0)])
+                else:
+                    d = [[("RD", j, ph + 1, i)] for i in range(4)]
+                    phase("R", order[ph], j, ph, s, add_us, d[3], d[1] + d[2], d[2], d[1], d[0])
+    add(("MA",), ("M",), 0.05, (), (), [(X, 1, 8192, ("m0",)), (X, -1, 8192, ("m1",))])
+    add(("MB",), ("M",), 0.05, [("MA",)], [("m0",), ("m1",)], [(X, 1, 8192, ("m2",))])
+    add(("MC",), ("M",), 0.05, [("MB",)], [("m2",)], [(Z, 1, 32768, ("m3",)), (Z, -1, 32768, ("m4",))])
+    add(("MD",), ("M",), 0.05, [("MC",)], [("m3",), ("m4",)], [(Z, 1, 32768, ("m5",))])
+    add(("META",), ("META",), COST["META"], [("MD",)], [("m5",)])
     for q in range(NP):
         add(("SB", q), ("SB", q), COST["SB"], [("META",)])
-    add(("HID",), ("HID",), COST["HID"], [("GU", j) for j in range(NP)])
+    for e in range(4):
+        add(("HID", e), ("HID", e), COST["HID"] / 4, [("GU", first[NP - 1], e)])
     return t
 
 
@@ -113,22 +162,27 @@
             return (0, home[g[1]][g[2]], g[3], g[4])
         if g[0] == "CBS":
             return (0, home[g[1]][2], 9, 0)
+        if g[0] == "M":
+            return (0, -8, 0, 0)
         if g[0] in ("META", "SB", "SLOT"):
             return (1, 0, 0, 0)
         if g[0] in ("SEL", "GU"):
-            return (2, first[g[1]], g[0] == "GU", 0)
+            return (2, first.index(g[1]), g[0] == "GU", 0)
         if g[0] == "HID":
             return (2, 50, 0, 0)
-        return (2, 100 + second[g[1]], g[0] == "CB", 0)
+        if g[0] == "CB":
+            return (2, 51, 0, 0)
+        return (2, 100 + second.index(g[1]), 0, g[2])
 
     return rank
 
 
 def plan(t, rank, backlog, trace=None):
     rate, lat = 46.6e3, 2.4
-    arrive = {("meta",): 5.0, ("pd",): 54.0}
+    arrive = {("pd",): 54.0}
     for j in range(NP):
         arrive[("pw", j)] = 8.5 + 4.5 * j
+    ids = {k: i for i, k in enumerate(sorted(t, key=lambda k: tuple(str(v) for v in k)))}
     left = {k: len(v[2]) for k, v in t.items()}
     after = {}
     for k, v in t.items():
@@ -148,14 +202,14 @@
                     when = max(when, free.get((a, d), 0.0) - backlog)
             if when <= now + 1e-9:
                 p = rank(group)
-                if best is None or (p, k) < best:
-                    best = (p, k)
+                if best is None or (p, ids[k]) < best[:2]:
+                    best = (p, ids[k], k)
             elif when < later:
                 later = when
         if best is None:
             now = later
             continue
-        k = best[1]
+        k = best[2]
         avail.remove(k)
         _, cost, _, _, sends = t[k]
         now += cost
@@ -175,40 +229,40 @@
 
 def schedule():
     trace = []
-    plan(tasks_of(ORDERS, BACK), priority(THERE, HOME, FIRST, SECOND), BACKLOG, trace)
-    gu = [k[1] for _, k in trace if k[0] == "GU"]
-    dn = [k[1] for _, k in trace if k[0] == "DN"]
-    out, early = [], [(14.0, gu[0]), (19.0, gu[1])]
+    plan(tasks_of(ORDERS, BACK, FIRST, SECOND), priority(THERE, HOME, FIRST, SECOND), BACKLOG, trace)
+    out, early = [], [(14.0, FIRST[0]), (19.0, FIRST[1])]
     for when, k in trace:
         while early and when >= early[0][0]:
             out.append(("LW", early.pop(0)[1]))
         out.append(k)
-        if k[0] == "GU":
-            i = gu.index(k[1]) + 2
-            out += [("LW", gu[i])] if i < NP else [("DW", dn[i - NP])]
-        if k[0] == "DN" and dn.index(k[1]) + 2 < NP:
-            out.append(("DW", dn[dn.index(k[1]) + 2]))
-    return out, gu, dn
-
-
-SCHEDULE, GU_ORDER, DN_ORDER = schedule()
+        if k[0] == "GU" and k[2] in (None, 3):
+            i = FIRST.index(k[1]) + 2
+            out += [("LW", FIRST[i])] if i < NP else [("DW", SECOND[i - NP])]
+        if k[0] == "DN" and k[2] in (None, 3) and SECOND.index(k[1]) + 2 < NP:
+            out.append(("DW", SECOND[SECOND.index(k[1]) + 2]))
+    return out
+
+
+SCHEDULE = schedule()
 SLOTTED = [j for j in range(NP) if ORDERS[j][2] == Y]
 PLAIN = [j for j in range(NP) if ORDERS[j][2] != Y]
+PLAIN_TURN = {j: i % 2 for i, j in enumerate(k for k in FIRST if k in PLAIN)}
+BACK_PLAIN = [j for j in SECOND if ORDERS[j][2] != Y]
 
 
 def unit(ph, s):
-    return ph + s
+    return sum(SPLIT[:ph]) + s
 
 
 def half_shape(j, order, ph):
     if j in SLOTTED and ph == 2:
         return (192, 128)
-    full = order[:min(ph, 1)]
+    full = order[:1] if ph == 2 else ()
     return (4 if X in full else 1, 4 if Z in full else 1, 64, 512 if Y in full else 128)
 
 
-def kernel(tok, meta, gw, uw, dw, out, pw, pd, t_ref, ts_ref, xs_ref, ys_ref, w_ref, d_ref, x_ref, acc, hid, y_ref,
-           s_ref, st_ref, ps, rk, pr, mb, ga, gb, gc, gs, ra, rc, rs, tok_sem, meta_send, meta_recv, meta_own,
+def kernel(tok, ids_t, prob_t, gw, uw, dw, out, pw, pd, t_ref, ts_ref, xs_ref, ys_ref, w_ref, d_ref, x_ref, acc, hid, y_ref,
+           s_ref, st_ref, ps, rk, pr, mbi, mbp, ga, gb, gc, gs, ra, rc, rs, tok_sem, meta_send, meta_recv, meta_own,
            pw_send, pw_recv, pd_send, pd_recv, w_sem, d_sem, *rb):
     ep = lax.axis_index("ep")
     y = lax.axis_index("etp")
@@ -221,11 +275,6 @@
         return {"ep": c[X] * 8 + c[Z] * 2 + core, "etp": c[Y]}
 
     partner = {"ep": x * 8 + z * 2 + (1 - core), "etp": y}
-    plane = [
-        {"ep": ((x + dx) % 4) * 8 + ((z + dz) % 4) * 2 + core, "etp": y}
-        for dx in range(4) for dz in range(4) if dx or dz
-    ]
-
     def lanes(i, n=1):
         return pl.ds(pl.multiple_of(i * 128, 128), 128 * n)
 
@@ -235,12 +284,13 @@
         own_tok.append(pltpu.make_async_copy(tok.at[:, pl.ds(j * 128, 128)], dst, tok_sem.at[j]))
     for c in own_tok:
         c.start()
-    g = x * 4 + z
-    own_meta = pltpu.make_async_copy(meta, mb.at[g], meta_own)
-    own_meta.start()
+    tables = ((ids_t, mbi), (prob_t, mbp))
+    own_meta = [pltpu.make_async_copy(src, dst.at[x, z], meta_own.at[i]) for i, (src, dst) in enumerate(tables)]
+    for c in own_meta:
+        c.start()
 
     barrier = pltpu.get_barrier_semaphore()
-    greet = plane + [at(Y, 1), at(Y, -1), partner]
+    greet = [at(a, d) for a in (X, Y, Z) for d in (1, -1)] + [partner]
     for d in greet:
         pl.semaphore_signal(barrier, inc=1, device_id=d, device_id_type=MESH)
     pl.semaphore_wait(barrier, len(greet))
@@ -257,9 +307,10 @@
 
     def spot(order, ph, pos, sub):
         p = list(own)
-        if ph >= 1:
+        if ph == 1:
+            p[order[0]] = place(order[0], SUB[sub])
+        if ph == 2:
             p[order[0]] = None
-        if ph == 2:
             p[order[1]] = place(order[1], SUB[sub])
         p[order[ph]] = pos
         return p
@@ -276,8 +327,11 @@
         cols = pl.ds(0, 512) if p[Y] is None else lanes(p[Y], many if a == Y else 1)
         return t_ref.at[PLAIN.index(j), ix, iz, rows, cols]
 
+    landed = set()
+
     def run_as(j, ph, s, first):
-        if ph == 0 and first:
+        if first and j not in landed:
+            landed.add(j)
             own_tok[j].wait()
         o = ORDERS[j]
         a, u = o[ph], unit(ph, s)
@@ -285,8 +339,8 @@
         for half, sign in ((0, 1), (1, -1)) if first else ((1, 1), (0, -1)):
             if first:
                 sem = ga.at[j, u, half]
-            elif ph == 1:
-                sem = gb.at[j, half]
+            elif ph < 2:
+                sem = gb.at[j, u, half]
             else:
                 sem = gc.at[j, u]
             h = slab(o, j, ph, s, p, half)
@@ -301,38 +355,70 @@
 
     def run_ab(j, ph, s, sign):
         half = 1 if sign > 0 else 0
-        wait(slab(ORDERS[j], j, ph, s, place(ORDERS[j][ph], -sign), half), gb.at[j, half])
+        wait(slab(ORDERS[j], j, ph, s, place(ORDERS[j][ph], -sign), half), gb.at[j, unit(ph, s), half])
 
     def run_ad(j, ph, s):
-        wait(slab(ORDERS[j], j, ph, s, 0, None, 1 if ph == 1 else 2), gc.at[j, unit(ph, s)])
+        wait(slab(ORDERS[j], j, ph, s, 0, None, 1 if ph < 2 else 2), gc.at[j, unit(ph, s)])
 
     def run_lw(j):
         wait(pw.at[j], pw_recv.at[j])
-        slot = GU_ORDER.index(j) % 2
+        slot = FIRST.index(j) % 2
         for e in range(2):
             for m, src in ((0, gw), (1, uw)):
                 s = pw.at[j, m] if e else src.at[:, :, j]
                 pltpu.make_async_copy(s, w_ref.at[slot, pl.ds(2 * e, 2), :, :, pl.ds(m * 384, 384)], w_sem.at[slot]).start()
 
     def run_dw(j):
-        if j == DN_ORDER[0]:
+        if j == SECOND[0]:
             wait(pd, pd_recv)
-        slot = DN_ORDER.index(j) % 2
+        slot = SECOND.index(j) % 2
         for e, src in ((0, dw), (1, pd)):
             for k in range(4):
                 pltpu.make_async_copy(
                     src.at[:, :, pl.ds(k * 1024 + j * 128, 128)],
                     d_ref.at[slot, pl.ds(2 * e, 2), :, pl.ds(k * 128, 128)], d_sem.at[slot]).start()
 
+    def table(dst, step, pos):
+        return dst.at[pl.ds(pos, 1), pl.ds(z, 1)] if step < 3 else dst.at[:, pl.ds(pos, 1)]
+
+    def send_meta(step, pos, axis, sign):
+        for i, (_, dst) in enumerate(tables):
+            ref = table(dst, step, pos)
+            remote(ref, ref, meta_send.at[i, step], meta_recv.at[i, step], at(axis, sign))
+
+    def wait_meta(step):
+        for i, (_, dst) in enumerate(tables):
+            wait(table(dst, step, 0), meta_recv.at[i, step])
+
+    def run_ma():
+        for c in own_meta:
+            c.wait()
+        send_meta(0, x, X, 1)
+        send_meta(1, x, X, -1)
+
+    def run_mb():
+        wait_meta(0)
+        wait_meta(1)
+        send_meta(2, place(X, -1), X, 1)
+
+    def run_mc():
+        wait_meta(2)
+        send_meta(3, z, Z, 1)
+        send_meta(4, z, Z, -1)
+
+    def run_md():
+        wait_meta(3)
+        wait_meta(4)
+        send_meta(5, place(Z, -1), Z, 1)
+
     def run_meta():
-        own_meta.wait()
-        wait(mb.at[pl.ds(0, 15)], meta_recv)
-        ids = mb[:, 0:8, :]
-        probs = mb[:, 8:16, :]
+        wait_meta(5)
+        ids = mbi[...].reshape(16, 8, 128)
+        probs = mbp[...].reshape(16, 8, 128)
         chip = (x * 4 + z) * 4
         rows, prows = [], []
         for e in (chip + 2 * core, chip + 2 * core + 1, chip + 2 * (1 - core), chip + 2 * (1 - core) + 1):
-            hit = ids == e.astype(F32)
+            hit = ids == e
             rows.append(jnp.sum(jnp.where(hit, 1.0, 0.0), axis=1))
             prows.append(jnp.sum(jnp.where(hit, probs, 0.0), axis=1))
         ind = jnp.concatenate(rows, axis=0)
@@ -356,7 +442,8 @@
         full = jnp.concatenate(blocks, axis=0)
         s_ref[q] = full[:4 * PAIR].astype(BF16)
         st_ref[q] = full.T.astype(BF16)
-        y_ref[q, 4 * PAIR:, :] = jnp.zeros((256 - 4 * PAIR, 512), BF16)
+        for i in range(2):
+            y_ref[i, q, 4 * PAIR:, :] = jnp.zeros((256 - 4 * PAIR, 512), BF16)
         for i in range(len(SLOTTED)):
             ys_ref[i, q, 4 * PAIR:, :] = jnp.zeros((256 - 4 * PAIR, 128), BF16)
 
@@ -377,31 +464,31 @@
                     if slotted:
                         xs_ref[SLOTTED.index(j), e, rows, lanes(y)] = r[e * PAIR:(e + 1) * PAIR]
                     else:
-                        x_ref[e, rows, :] = r[e * PAIR:(e + 1) * PAIR]
+                        x_ref[PLAIN_TURN[j], e, rows, :] = r[e * PAIR:(e + 1) * PAIR]
             return carry
 
         lax.fori_loop(0, 2, step, 0)
 
-    def run_gu(j):
-        slot = GU_ORDER.index(j) % 2
-        wait(w_ref.at[slot], w_sem.at[slot])
+    def run_gu(j, part):
+        slot = FIRST.index(j) % 2
+        if part in (None, 0):
+            wait(w_ref.at[slot], w_sem.at[slot])
 
         def step(e, carry):
-            rows = xs_ref[SLOTTED.index(j), e] if j in SLOTTED else x_ref[e]
+            rows = xs_ref[SLOTTED.index(j), e] if j in SLOTTED else x_ref[PLAIN_TURN[j], e]
             for n in range(3):
                 w = w_ref[slot, e, :, :, n * 256:(n + 1) * 256].reshape(512, 256)
                 r = jnp.dot(rows, w, preferred_element_type=F32)
-                if j == GU_ORDER[0]:
+                if j == FIRST[0]:
                     acc[e, :, n * 256:(n + 1) * 256] = r
                 else:
                     acc[e, :, n * 256:(n + 1) * 256] += r
             return carry
 
-        lax.fori_loop(0, 4, step, 0)
-
-    def run_hid():
-        def step(i, carry):
-            e, k = i // 4, i % 4
+        lax.fori_loop(0, 4, step, 0) if part is None else step(part, 0)
+
+    def run_hid(e):
+        def step(k, carry):
             rows = pl.ds(pl.multiple_of(k * 96, 16), 96)
             w = ps[e, rows, :]
             for n in range(3):
@@ -410,13 +497,14 @@
                 hid[e, rows, n * 128:(n + 1) * 128] = h.astype(BF16)
             return carry
 
-        lax.fori_loop(0, 16, step, 0)
-
-    def run_dn(j):
-        slot = DN_ORDER.index(j) % 2
-        wait(d_ref.at[slot], d_sem.at[slot])
+        lax.fori_loop(0, 4, step, 0)
+
+    def run_dn(j, part):
+        slot = SECOND.index(j) % 2
         slotted = j in SLOTTED
-        if slotted:
+        if part in (None, 0):
+            wait(d_ref.at[slot], d_sem.at[slot])
+        if slotted and part in (None, 0):
             for s in range(4):
                 wait(slab(ORDERS[j], j, 2, s, 0, None, 3), gs.at[j, unit(2, s)])
 
@@ -426,21 +514,21 @@
                 xs_ref[SLOTTED.index(j), e] = r
             else:
                 for q in range(NP):
-                    y_ref[q, pl.ds(pl.multiple_of(e * PAIR, 16), PAIR), :] = r[q * PAIR:(q + 1) * PAIR]
+                    y_ref[BACK_PLAIN.index(j) % 2, q, pl.ds(pl.multiple_of(e * PAIR, 16), PAIR), :] = r[q * PAIR:(q + 1) * PAIR]
             return carry
 
-        lax.fori_loop(0, 4, step, 0)
+        lax.fori_loop(0, 4, step, 0) if part is None else step(part, 0)
 
     def run_cb(j):
         slotted = j in SLOTTED
-        for ph, s in ((0, 0), (1, 0)) + (() if slotted else tuple((2, s) for s in range(4))):
+        for ph, s in ((ph, s) for ph in range(2 if slotted else 3) for s in range(SPLIT[ph])):
             wait(slab(ORDERS[j], j, ph, s, 0, None, 3), gs.at[j, unit(ph, s)])
 
         def step(i, carry):
             for k in range(4):
                 q = 4 * i + k
                 gx, gz = 2 * i + k // 2, slice((k % 2) * 2, (k % 2) * 2 + 2)
-                rows = ys_ref[SLOTTED.index(j), q] if slotted else y_ref[q]
+                rows = ys_ref[SLOTTED.index(j), q] if slotted else y_ref[BACK_PLAIN.index(j) % 2, q]
                 r = jnp.dot(st_ref[q], rows, preferred_element_type=F32).astype(BF16)
                 if slotted:
                     ts_ref[SLOTTED.index(j), gx, gz] = r.reshape(2, 128, 128)
@@ -518,13 +606,11 @@
         add_into(j, ph, s, p, 1, (2, 5), True)
 
     started = 0
-    while SCHEDULE[started][0] in ("AS0", "AS1"):
+    while SCHEDULE[started][0] in ("AS0", "AS1", "MA"):
         k = SCHEDULE[started]
-        run_as(*k[1:], k[0] == "AS0")
+        run_ma() if k[0] == "MA" else run_as(*k[1:], k[0] == "AS0")
         started += 1
-    for d in plane:
-        remote(meta, mb.at[g], meta_send, meta_recv, d)
-    for j in GU_ORDER:
+    for j in FIRST:
         remote(gw.at[:, :, j], pw.at[j, 0], pw_send, pw_recv.at[j], partner)
         remote(uw.at[:, :, j], pw.at[j, 1], pw_send, pw_recv.at[j], partner)
     remote(dw, pd, pd_send, pd_recv, partner)
@@ -536,22 +622,23 @@
         "LW": run_lw, "DW": run_dw, "SEL": run_sel, "GU": run_gu, "DN": run_dn, "CB": run_cb,
         "RS0": lambda *k: run_rs(*k, True), "RS1": lambda *k: run_rs(*k, False),
         "RF+": lambda *k: run_rf(*k, 1), "RF-": lambda *k: run_rf(*k, -1), "RD": run_rd,
-        "META": run_meta, "SB": run_sb, "HID": run_hid,
+        "MA": run_ma, "MB": run_mb, "MC": run_mc, "MD": run_md, "META": run_meta, "SB": run_sb, "HID": run_hid,
     }
     for task in SCHEDULE[started:]:
         runs[task[0]](*task[1:])
 
     for j in range(NP):
         for ph in range(3):
-            for s in range(4 if ph == 2 else 1):
+            for s in range(SPLIT[ph]):
                 wait(slab(BACK[j], j, ph, s, 0, None, 3), rs.at[j, unit(ph, s)])
-    wait(mb.at[pl.ds(0, 15)], meta_send)
+    for i, (_, dst) in enumerate(tables):
+        for step in range(6):
+            wait(table(dst, step, 0), meta_send.at[i, step])
     wait(pw, pw_send)
     wait(pd, pd_send)
 
 
 def body(tokens, expert_ids, gate_prob, gate_weight, up_weight, down_weight):
-    meta = jnp.concatenate([expert_ids.T.astype(F32), gate_prob.T], axis=0)
     gw = gate_weight.reshape(2, 4, NP, 128, 384)
     uw = up_weight.reshape(2, 4, NP, 128, 384)
     hbm = pl.BlockSpec(memory_space=pl.ANY)
@@ -564,21 +651,22 @@
         pltpu.VMEM((ns, 8, 256, 128), BF16),
         pltpu.VMEM((2, 4, 4, 128, 768), BF16),
         pltpu.VMEM((2, 4, 384, 512), BF16),
-        pltpu.VMEM((4, 384, 512), BF16),
+        pltpu.VMEM((2, 4, 384, 512), BF16),
         pltpu.VMEM((4, 384, 768), F32),
         pltpu.VMEM((4, 384, 384), BF16),
-        pltpu.VMEM((8, 256, 512), BF16),
+        pltpu.VMEM((2, 8, 256, 512), BF16),
         pltpu.VMEM((8, 4 * PAIR, 256), BF16),
         pltpu.VMEM((8, 256, 256), BF16),
         pltpu.VMEM((4, 384, 128), F32),
         pltpu.VMEM((64, 128), F32),
         pltpu.VMEM((64, 128), F32),
-        pltpu.VMEM((16, 16, 128), F32),
-        dma((NP, 6, 2)), dma((NP, 2)), dma((NP, 6)), dma((NP, 6)),
-        dma((NP, 6, 2)), dma((NP, 6)), dma((NP, 6)),
-        dma((NP,)), dma, dma, dma, dma, dma((NP,)), dma, dma, dma((2,)), dma((2,)),
+        pltpu.VMEM((4, 4, 8, 128), jnp.int32),
+        pltpu.VMEM((4, 4, 8, 128), F32),
+        dma((NP, 9, 2)), dma((NP, 5, 2)), dma((NP, 9)), dma((NP, 9)),
+        dma((NP, 9, 2)), dma((NP, 9)), dma((NP, 9)),
+        dma((NP,)), dma((2, 6)), dma((2, 6)), dma((2,)), dma, dma((NP,)), dma, dma, dma((2,)), dma((2,)),
     ] + [
-        pltpu.VMEM((4 if ph == 2 else 1, 6) + half_shape(j, BACK[j], ph), BF16)
+        pltpu.VMEM((SPLIT[ph], 6) + half_shape(j, BACK[j], ph), BF16)
         for j in range(NP) for ph in range(3)
     ]
     return pl.pallas_call(
@@ -589,11 +677,11 @@
             jax.ShapeDtypeStruct((NP, 2, 2, 4, 128, 384), BF16),
             jax.ShapeDtypeStruct((2, 384, 4096), BF16),
         ),
-        in_specs=[hbm] * 5,
+        in_specs=[hbm] * 6,
         out_specs=(pl.BlockSpec(memory_space=pltpu.VMEM), hbm, hbm),
         scratch_shapes=scratch,
         compiler_params=pltpu.CompilerParams(collective_id=0, has_side_effects=True, vmem_limit_bytes=67043328),
-    )(tokens, meta, gw, uw, down_weight)[0]
+    )(tokens, expert_ids.T, gate_prob.T, gw, uw, down_weight)[0]
 
 
 def solution(mesh):

time: 150 us -> 143 us (0.953)
  Pallas kernels: 146 us -> 141 us
  other arithmetic: 1.97 us -> 0 us
    pallas_call x1, Pallas kernels: 146 us -> 141 us  [body(): pl.pallas_call(kernel, name='moe', out_shape=(jax.ShapeDtypeStruct((128,...]
where the time goes in v3:
time: 143 us
  Pallas kernels  141 us (99%)
  local copies, waits for them, and re-layouts  1.67 us (1%)
    pallas_call x1, Pallas kernels, body(): pl.pallas_call(kernel, name='moe', out_shape=(jax.ShapeDtypeStruct((128,...  141 us

profile of v3, /device:TPU:0, one launch (start us, length us, event | category | flops | bytes accessed | tf_op | source)
XLA Modules:
  0.0 142.5 jit_solution(12778631804795686510)
XLA Ops:
  0.0 140.8 %moe.1 = (bf16[128,1024]{1,0:T(8,128)(2,1)}, bf16[8,2,2,4,128,384]{5,4,3,2,1,0:T(8,128)(2,1)}, bf16[2,384,4096]{2,1,0:T(8,128)(2,1)}) custom-call(bf16[128,1024]{1,0:T(8,128)(2,1)} %tok.1, s32[8,128]{1,0:T(8,128)} %bitcast.6, f32[8,128]{1,0:T(8,128)} %bitcast.7, bf16[2,4,8,128,384]{4,3,2,1,0:T(8,128)(2,1)} %bitcast.4, bf16[2,4,8,128,384]{4,3,2,1,0:T(8,128)(2,1)} %bitcast.5, ...), custom_call_target="tpu_custom_call" | custom-call | tf_op jit(solution)/shard_map/moe/pallas_call | solution.py:672
  140.8 1.7 %copy.8 = bf16[128,1024]{1,0:T(8,128)(2,1)} copy(bf16[128,1024]{1,0:T(8,128)(2,1)} %get-tuple-element.6) | data formatting | bytes 524288

commit v4 on v3

--- a/solution.py
+++ b/solution.py
@@ -18,30 +18,31 @@
     (Z, Y, X),
     (Z, X, Y),
     (X, Y, Z),
+    (X, Y, Z),
+    (Z, X, Y),
+    (Z, Y, X),
     (Z, X, Y),
     (Y, X, Z),
-    (Z, Y, X),
-    (Z, X, Y),
-    (X, Y, Z),
 )
 BACK = (
     (X, Y, Z),
     (Z, X, Y),
     (X, Y, Z),
-    (Z, X, Y),
-    (Y, X, Z),
     (Z, Y, X),
     (Z, X, Y),
     (Z, Y, X),
+    (Z, X, Y),
+    (Y, X, Z),
 )
-THERE = ((2, 9, 11), (5, 2, 0), (10, 4, 2), (10, 3, 2), (10, 8, 2), (2, 3, 12), (10, 11, 3), (1, 9, 6))
-HOME = ((3, 11, 11), (9, 4, 10), (5, 11, 7), (10, 3, 10), (1, 8, 11), (13, 11, 1), (7, 11, 10), (13, 11, 7))
+THERE = ((6, 0, 1), (2, 3, 2), (2, 3, 4), (0, 5, 5), (4, 4, 5), (5, 3, 7), (4, 6, 3), (5, 4, 6))
+HOME = ((2, 5, 5), (4, 4, 2), (6, 5, 5), (7, 5, 5), (6, 6, 1), (5, 5, 3), (7, 5, 4), (1, 4, 5))
 FIRST = (0, 1, 2, 3, 4, 5, 6, 7)
-SECOND = (2, 6, 5, 4, 7, 1, 3, 0)
+SECOND = (0, 6, 5, 3, 1, 4, 7, 2)
 BACKLOG = 2.0
 
 SPLIT = (1, 4, 4)
-COST = dict(SEL=0.76, SLOT=0.35, GU=1.9, HID=1.0, DN=1.45, CB=0.88, CBS=0.45, META=0.3, SB=0.12, ADD=0.12)
+COST = dict(SEL=0.76, SLOT=0.35, GU=1.9, HID=0.4, DN=1.45, CB=0.88, CBS=0.45, META=0.3, SB=0.12, ADD=0.12)
+FAST = 4
 
 
 def tasks_of(orders, back, first, second):
@@ -56,11 +57,11 @@
     def phase(tag, axis, j, ph, s, per, before, second=(), up=(), down=(), last=()):
         k = (j, ph, s)
         size = size_of(axis, ph)
-        v = 0.04 + per * size / 262144
+        v = 0.06 + per * size / 262144
         s0, s1, fp, fm = (tag + "S0",) + k, (tag + "S1",) + k, (tag + "F+",) + k, (tag + "F-",) + k
         group = (tag, j, ph, s if tag == "A" else 3 - s)
-        add(s0, group + (0,), 0.04, before, (), [(axis, 1, size, ("a+", tag) + k), (axis, -1, size, ("a-", tag) + k)])
-        add(s1, group + (1,), 0.04, [s0, *second], (), [(axis, 1, size, ("b+", tag) + k), (axis, -1, size, ("b-", tag) + k)])
+        add(s0, group + (0,), 0.06, before, (), [(axis, 1, size, ("a+", tag) + k), (axis, -1, size, ("a-", tag) + k)])
+        add(s1, group + (1,), 0.06, [s0, *second], (), [(axis, 1, size, ("b+", tag) + k), (axis, -1, size, ("b-", tag) + k)])
         add(fp, group + (-1,), v, [s1, *up], [("a+", tag) + k], [(axis, 1, size, ("c+", tag) + k)])
         add(fm, group + (-1,), v, [s1, *down], [("a-", tag) + k], [(axis, -1, size, ("c-", tag) + k)])
         g = group + (-2,)
@@ -77,14 +78,21 @@
     def parts(split):
         return range(4) if split else (None,)
 
-    def share(kind, e):
-        return COST[kind] if e is None else COST[kind] / 4
+    def share(kind, j, e):
+        fast = j == first[-1] if kind in ("SEL", "GU") else second.index(j) < FAST
+        return COST[kind] * (0.75 if fast else 1.0) * (1.0 if e is None else 0.3)
+
+    def split_gu(j):
+        return j == first[-1] and orders[j][2] == Y
+
+    def split_dn(j):
+        return second.index(j) < 2 and orders[j][2] == Y
 
     def gu_end(j):
-        return ("GU", j, 3 if j == first[-1] else None)
+        return ("GU", j, 3 if split_gu(j) else None)
 
     def dn_end(j):
-        return ("DN", j, 3 if second.index(j) < 2 else None)
+        return ("DN", j, 3 if split_dn(j) else None)
 
     sb = [("SB", q) for q in range(NP)]
     plain = [j for j in first if orders[j][2] != Y]
@@ -110,31 +118,33 @@
             add(("SEL", j), ("SLOT", j), COST["SLOT"], every("AD", j, 1) + sb)
         else:
             i = plain.index(j)
-            add(("SEL", j), ("SEL", j), COST["SEL"], every("AD", j, 2) + sb + ([gu_end(plain[i - 2])] if i > 1 else []))
-        for e in parts(j == first[-1]):
+            add(("SEL", j), ("SEL", j), share("SEL", j, None), every("AD", j, 2) + sb + ([gu_end(plain[i - 2])] if i > 1 else []))
+        for e in parts(split_gu(j)):
             here = every("AD", j, 2) if e is None else [("AD", j, 2, e)]
             prev = [("GU", j, e - 1)] if e else turn
-            add(("GU", j, e), ("GU", j, e or 0), share("GU", e), [("SEL", j)] + (here if slot else []) + prev, [("pw", at)])
+            add(("GU", j, e), ("GU", j, e or 0), share("GU", j, e), [("SEL", j)] + (here if slot else []) + prev, [("pw", at)])
         at = second.index(j)
         i = 0 if slot else back_plain.index(j)
-        for e in parts(at < 2):
+        for e in parts(split_dn(j)):
             prev = [("DN", j, e - 1)] if e else []
-            if at == 1:
-                prev.append(("DN", second[0], e))
+            if at and split_dn(j) and split_dn(second[at - 1]):
+                prev.append(("DN", second[at - 1], e))
+            elif at and not split_dn(j):
+                prev.append(dn_end(second[at - 1]))
             if at > 1:
-                prev += [dn_end(second[at - 1]), dn_end(second[at - 2])]
+                prev.append(dn_end(second[at - 2]))
             if not slot and i > 1:
                 prev.append(("CB", back_plain[i - 2]))
-            add(("DN", j, e), ("DN", j, e or 0), share("DN", e), [("HID", 3 if e is None else e)] + prev, [("pd",)])
+            add(("DN", j, e), ("DN", j, e or 0), share("DN", j, e), [("HID", 3 if e is None else e)] + prev, [("pd",)])
         order, add_us = back[j], COST["ADD"]
         if slot:
             add(("CB", j), ("CBS", j), COST["CBS"], every("RD", j, 2))
         else:
-            add(("CB", j), ("CB", j), COST["CB"], [dn_end(j)])
+            add(("CB", j), ("CB", j), share("CB", j, None), [dn_end(j)])
         for ph in (2, 1, 0):
             for s in range(SPLIT[ph] - 1, -1, -1):
                 if ph == 2:
-                    phase("R", order[2], j, 2, s, add_us, [(("DN", j, s) if at < 2 else dn_end(j)) if slot else ("CB", j)])
+                    phase("R", order[2], j, 2, s, add_us, [(("DN", j, s) if split_dn(j) else dn_end(j)) if slot else ("CB", j)])
                 elif ph == 1 and slot:
                     phase("R", order[1], j, 1, s, add_us, [("CB", j)])
                 elif SPLIT[ph + 1] == 1:
@@ -150,7 +160,7 @@
     for q in range(NP):
         add(("SB", q), ("SB", q), COST["SB"], [("META",)])
     for e in range(4):
-        add(("HID", e), ("HID", e), COST["HID"] / 4, [("GU", first[NP - 1], e)])
+        add(("HID", e), ("HID", e), COST["HID"] / 4, [("GU", first[-1], e) if split_gu(first[-1]) else gu_end(first[-1])])
     return t
 
 
@@ -166,19 +176,21 @@
             return (0, -8, 0, 0)
         if g[0] in ("META", "SB", "SLOT"):
             return (1, 0, 0, 0)
-        if g[0] in ("SEL", "GU"):
+        if g[0] in ("SEL", "GU") and g[1] != first[-1]:
             return (2, first.index(g[1]), g[0] == "GU", 0)
-        if g[0] == "HID":
-            return (2, 50, 0, 0)
+        if g[0] == "SEL":
+            return (2, 49, 0, 0)
+        if g[0] in ("GU", "HID"):
+            return (2, 50, g[-1], g[0] == "HID")
         if g[0] == "CB":
             return (2, 51, 0, 0)
-        return (2, 100 + second.index(g[1]), 0, g[2])
+        return (2, 60 + second.index(g[1]), g[2], 0)
 
     return rank
 
 
 def plan(t, rank, backlog, trace=None):
-    rate, lat = 46.6e3, 2.4
+    rate, lat = 46.6e3, 2.9
     arrive = {("pd",): 54.0}
     for j in range(NP):
         arrive[("pw", j)] = 8.5 + 4.5 * j
@@ -447,6 +459,16 @@
         for i in range(len(SLOTTED)):
             ys_ref[i, q, 4 * PAIR:, :] = jnp.zeros((256 - 4 * PAIR, 128), BF16)
 
+    def loop(n, step, unrolled):
+        if unrolled:
+            for i in range(n):
+                step(i, 0)
+        else:
+            lax.fori_loop(0, n, step, 0)
+
+    def fast(j):
+        return SECOND.index(j) < FAST
+
     def run_sel(j):
         slotted = j in SLOTTED
 
@@ -467,7 +489,7 @@
                         x_ref[PLAIN_TURN[j], e, rows, :] = r[e * PAIR:(e + 1) * PAIR]
             return carry
 
-        lax.fori_loop(0, 2, step, 0)
+        loop(2, step, j == FIRST[-1])
 
     def run_gu(j, part):
         slot = FIRST.index(j) % 2
@@ -485,7 +507,7 @@
                     acc[e, :, n * 256:(n + 1) * 256] += r
             return carry
 
-        lax.fori_loop(0, 4, step, 0) if part is None else step(part, 0)
+        loop(4, step, j == FIRST[-1]) if part is None else step(part, 0)
 
     def run_hid(e):
         def step(k, carry):
@@ -497,7 +519,7 @@
                 hid[e, rows, n * 128:(n + 1) * 128] = h.astype(BF16)
             return carry
 
-        lax.fori_loop(0, 4, step, 0)
+        loop(4, step, True)
 
     def run_dn(j, part):
         slot = SECOND.index(j) % 2
@@ -517,7 +539,7 @@
                     y_ref[BACK_PLAIN.index(j) % 2, q, pl.ds(pl.multiple_of(e * PAIR, 16), PAIR), :] = r[q * PAIR:(q + 1) * PAIR]
             return carry
 
-        lax.fori_loop(0, 4, step, 0) if part is None else step(part, 0)
+        loop(4, step, fast(j)) if part is None else step(part, 0)
 
     def run_cb(j):
         slotted = j in SLOTTED
@@ -536,7 +558,7 @@
                     t_ref[PLAIN.index(j), gx, gz] = r.reshape(2, 128, 512)
             return carry
 
-        lax.fori_loop(0, 2, step, 0)
+        loop(2, step, fast(j))
 
     def buf(j, ph, s):
         return rb[3 * j + ph].at[s]

time: 143 us -> 140 us (0.979)
  Pallas kernels: 141 us -> 138 us
    pallas_call x1, Pallas kernels: 141 us -> 138 us  [body(): pl.pallas_call(kernel, name='moe', out_shape=(jax.ShapeDtypeStruct((128,...]
where the time goes in v4:
time: 140 us
  Pallas kernels  138 us (99%)
  local copies, waits for them, and re-layouts  1.67 us (1%)
    pallas_call x1, Pallas kernels, body(): pl.pallas_call(kernel, name='moe', out_shape=(jax.ShapeDtypeStruct((128,...  138 us

profile of v4, /device:TPU:0, one launch (start us, length us, event | category | flops | bytes accessed | tf_op | source)
XLA Modules:
  0.0 139.9 jit_solution(2904846835921588096)
XLA Ops:
  0.0 138.3 %moe.1 = (bf16[128,1024]{1,0:T(8,128)(2,1)}, bf16[8,2,2,4,128,384]{5,4,3,2,1,0:T(8,128)(2,1)}, bf16[2,384,4096]{2,1,0:T(8,128)(2,1)}) custom-call(bf16[128,1024]{1,0:T(8,128)(2,1)} %tok.1, s32[8,128]{1,0:T(8,128)} %bitcast.6, f32[8,128]{1,0:T(8,128)} %bitcast.7, bf16[2,4,8,128,384]{4,3,2,1,0:T(8,128)(2,1)} %bitcast.4, bf16[2,4,8,128,384]{4,3,2,1,0:T(8,128)(2,1)} %bitcast.5, ...), custom_call_target="tpu_custom_call" | custom-call | tf_op jit(solution)/shard_map/moe/pallas_call | solution.py:694
  138.3 1.7 %copy.8 = bf16[128,1024]{1,0:T(8,128)(2,1)} copy(bf16[128,1024]{1,0:T(8,128)(2,1)} %get-tuple-element.6) | data formatting | bytes 524288

commit v5 on v4

--- a/solution.py
+++ b/solution.py
@@ -273,7 +273,7 @@
     return (4 if X in full else 1, 4 if Z in full else 1, 64, 512 if Y in full else 128)
 
 
-def kernel(tok, ids_t, prob_t, gw, uw, dw, out, pw, pd, t_ref, ts_ref, xs_ref, ys_ref, w_ref, d_ref, x_ref, acc, hid, y_ref,
+def kernel(tok, ids_t, prob_t, gw, uw, dw, result, pw, pd, out, out_sem, t_ref, ts_ref, xs_ref, ys_ref, w_ref, d_ref, x_ref, acc, hid, y_ref,
            s_ref, st_ref, ps, rk, pr, mbi, mbp, ga, gb, gc, gs, ra, rc, rs, tok_sem, meta_send, meta_recv, meta_own,
            pw_send, pw_recv, pd_send, pd_recv, w_sem, d_sem, *rb):
     ep = lax.axis_index("ep")
@@ -621,11 +621,17 @@
         add_into(j, ph, s, pos, half, (half,), False)
         remote(slab(o, j, ph, s, pos, half), b.at[4 + half], rs.at[j, u], rc.at[j, u], at(o[ph], sign))
 
+    def write_back(j):
+        cols = pl.ds(j * 128, 128)
+        return pltpu.make_async_copy(out.at[:, cols], result.at[:, cols], out_sem.at[j])
+
     def run_rd(j, ph, s):
         wait(buf(j, ph, s).at[pl.ds(2, 4)], rc.at[j, unit(ph, s)])
         p = own[BACK[j][ph]]
         add_into(j, ph, s, p, 0, (3, 4), True)
         add_into(j, ph, s, p, 1, (2, 5), True)
+        if ph == 0:
+            write_back(j).start()
 
     started = 0
     while SCHEDULE[started][0] in ("AS0", "AS1", "MA"):
@@ -656,6 +662,8 @@
     for i, (_, dst) in enumerate(tables):
         for step in range(6):
             wait(table(dst, step, 0), meta_send.at[i, step])
+    for j in range(NP):
+        write_back(j).wait()
     wait(pw, pw_send)
     wait(pd, pd_send)
 
@@ -667,6 +675,8 @@
     dma = pltpu.SemaphoreType.DMA
     ns = len(SLOTTED)
     scratch = [
+        pltpu.VMEM((128, 1024), BF16),
+        dma((NP,)),
         pltpu.VMEM((NP - ns, 4, 4, 128, 512), BF16),
         pltpu.VMEM((ns, 4, 4, 128, 128), BF16),
         pltpu.VMEM((ns, 4, 384, 512), BF16),
@@ -700,7 +710,7 @@
             jax.ShapeDtypeStruct((2, 384, 4096), BF16),
         ),
         in_specs=[hbm] * 6,
-        out_specs=(pl.BlockSpec(memory_space=pltpu.VMEM), hbm, hbm),
+        out_specs=(hbm, hbm, hbm),
         scratch_shapes=scratch,
         compiler_params=pltpu.CompilerParams(collective_id=0, has_side_effects=True, vmem_limit_bytes=67043328),
     )(tokens, expert_ids.T, gate_prob.T, gw, uw, down_weight)[0]

time: 140 us -> 140 us (level)
  no operation moved by 1% of the time
where the time goes in v5:
time: 140 us
  Pallas kernels  138 us (99%)
  local copies, waits for them, and re-layouts  1.67 us (1%)
    pallas_call x1, Pallas kernels, body(): pl.pallas_call(kernel, name='moe', out_shape=(jax.ShapeDtypeStruct((128,...  138 us

profile of v5, /device:TPU:0, one launch (start us, length us, event | category | flops | bytes accessed | tf_op | source)
XLA Modules:
  0.0 139.8 jit_solution(17494209861488068100)
XLA Ops:
  0.0 138.1 %moe.1 = (bf16[128,1024]{1,0:T(8,128)(2,1)}, bf16[8,2,2,4,128,384]{5,4,3,2,1,0:T(8,128)(2,1)}, bf16[2,384,4096]{2,1,0:T(8,128)(2,1)}) custom-call(bf16[128,1024]{1,0:T(8,128)(2,1)} %tok.1, s32[8,128]{1,0:T(8,128)} %bitcast.6, f32[8,128]{1,0:T(8,128)} %bitcast.7, bf16[2,4,8,128,384]{4,3,2,1,0:T(8,128)(2,1)} %bitcast.4, bf16[2,4,8,128,384]{4,3,2,1,0:T(8,128)(2,1)} %bitcast.5, ...), custom_call_target="tpu_custom_call" | custom-call | tf_op jit(solution)/shard_map/moe/pallas_call | solution.py:704
  138.1 1.7 %copy.8 = bf16[128,1024]{1,0:T(8,128)(2,1)} copy(bf16[128,1024]{1,0:T(8,128)(2,1)} %get-tuple-element.6) | data formatting | bytes 524288
